TPU v7x, 256 devices: a whole 4x4x8 slice. The times are simulated.
256 devices in a mesh: dp: 4 (over x), seq: 8 (over z_lo, core), head: 8 (over y, z_hi).
Axes of the slice: x: 4, y: 4, z: 8 (z_hi: 2, z_lo: 4; z = z_hi * 4 + z_lo), core: 2. Of those that a mesh axis runs over, the one named last changes fastest.
Arguments:
- q_lat: bfloat16 [12288, 8192], P(('dp', 'seq'), 'head'), may hold values from -160 to 160
- q_rope: bfloat16 [12288, 1024], P(('dp', 'seq'), 'head'), may hold values from -6 to 6
- grad_out: bfloat16 [12288, 8192], P(('dp', 'seq'), 'head'), may hold values from -6 to 6
- prefix_keys: bfloat16 [576, 2048], P(None, 'seq'), may hold values from -6 to 6
- comp_lengths: int32 [12], replicated, may hold values from 128 to 1024, as said below
- prefix_len: int32 [1], replicated, may hold values from 257 to 2048
Outputs:
- dq_lat: bfloat16 [12288, 8192], P(('dp', 'seq'), 'head')
- dq_rope: bfloat16 [12288, 1024], P(('dp', 'seq'), 'head')
- d_keys: float32 [576, 2048], P(None, ('seq', 'head'))
Inputs may be any that keep to these rules, and one draw needn't show every extreme that they name: `comp_lengths`: each a multiple of 128.
All inputs are finite; a program needn't handle non-finite values.
Results may differ from a plain program's by a relative error of at most 0.0089.
Values may be sent and summed in bfloat16 or wider, within the bound.
No kernel may reach another device: no remote copies, remote signals or barrier semaphores. Data moves between devices by JAX's collectives and lax.ppermute only.
A program may use at most 64 MiB of HBM per device.

v0:
```python
import jax
import jax.numpy as jnp
from jax import lax
from jax.sharding import PartitionSpec as P

DL = 512
DR = 64
CLEN = 1024


neg_value = -1e30


def from_everyone(value, axis):
    peers = lax.axis_size(axis)
    return lax.all_to_all(
        jnp.broadcast_to(value[None], (peers, *value.shape)), axis, 0, 0, tiled=True
    )


def joined_along(tiles, dim):
    tiles = jnp.moveaxis(tiles, 0, dim)
    dims = tiles.shape
    return tiles.reshape(*dims[:dim], dims[dim] * dims[dim + 1], *dims[dim + 2 :])


def gathered_copies(value, axis, dim):
    tiles = from_everyone(value, axis)
    return joined_along(tiles, dim)


def cut_along(value, dim, peers):
    before, after = (value.shape[:dim], value.shape[dim + 1 :])
    return jnp.moveaxis(value.reshape(*before, peers, -1, *after), dim, 0)


def sent_and_summed(value, axis, dim):
    peers = lax.axis_size(axis)
    tiles = lax.all_to_all(cut_along(value, dim, peers), axis, 0, 0, tiled=True)
    return jnp.sum(tiles.astype(jnp.float32), axis=0)


def of_everyone(value, axis):
    everything = from_everyone(value, axis)
    return jnp.sum(everything, axis=0)


def on_device(q_lat, q_rope, grad_out, prefix_keys, comp_lengths, prefix_len):
    tok_rows = q_lat.shape[0]
    heads_here = q_lat.shape[1] // DL
    rows = tok_rows * heads_here
    scale = (DL + DR) ** (-0.5)
    tok_ids = lax.axis_index(("dp", "seq")) * tok_rows + jnp.arange(tok_rows, dtype=jnp.int32)
    comp_ids = tok_ids // CLEN
    table = jnp.arange(comp_lengths.shape[0], dtype=jnp.int32)
    length = jnp.sum(
        jnp.where(comp_ids[:, None] == table[None, :], comp_lengths[None, :], 0), axis=1
    )
    valid = tok_ids % CLEN < length
    query_lat = q_lat.reshape(rows, DL)
    query_rope = q_rope.reshape(rows, DR)
    upstream = jnp.where(
        jnp.repeat(valid, heads_here)[:, None],
        grad_out.reshape(rows, DL),
        jnp.zeros((), jnp.bfloat16),
    )
    limit = prefix_len[0]
    total_keys = prefix_keys.shape[1] * lax.axis_size("seq")
    contract_last = (((1,), (1,)), ((), ()))
    contract_first = (((0,), (0,)), ((), ()))

    def scores_of(piece):
        key_lat = piece[:DL]
        key_rope = piece[DL:]
        scores = (
            jnp.dot(query_lat, key_lat, preferred_element_type=jnp.float32)
            + jnp.dot(query_rope, key_rope, preferred_element_type=jnp.float32)
        ) * scale
        keep = jnp.arange(piece.shape[1], dtype=jnp.int32) < limit
        dprob = jnp.dot(upstream, key_lat, preferred_element_type=jnp.float32)
        return (key_lat, key_rope, scores, keep[None, :], dprob)

    def make_backward(peak, total, delta):

        def backward_step(carry, piece, start):
            key_lat, key_rope, scores, keep, dprob = scores_of(piece)
            prob = jnp.where(
                keep,
                jnp.exp(jnp.where(keep, scores, neg_value) - peak[:, None]) / total[:, None],
                0.0,
            )
            dscore = prob * (dprob - delta[:, None])
            prob_b = prob.astype(jnp.bfloat16)
            dscore_b = dscore.astype(jnp.bfloat16)
            grad_lat = lax.dot_general(
                dscore_b, key_lat, contract_last, preferred_element_type=jnp.float32
            )
            grad_rope = lax.dot_general(
                dscore_b, key_rope, contract_last, preferred_element_type=jnp.float32
            )
            term_lat = lax.dot_general(
                upstream, prob_b, contract_first, preferred_element_type=jnp.float32
            ) + scale * lax.dot_general(
                query_lat, dscore_b, contract_first, preferred_element_type=jnp.float32
            )
            term_rope = scale * lax.dot_general(
                query_rope, dscore_b, contract_first, preferred_element_type=jnp.float32
            )
            update = jnp.concatenate([term_lat, term_rope], axis=0)
            return (grad_lat, grad_rope, update)

        return backward_step

    grads_init = (
        jnp.zeros((rows, DL), jnp.float32),
        jnp.zeros((rows, DR), jnp.float32),
        jnp.zeros((DL + DR, total_keys), jnp.float32),
    )
    peak = jnp.full((rows,), neg_value, jnp.float32)
    total = jnp.zeros((rows,), jnp.float32)
    key_lat, key_rope, scores, keep, dprob = scores_of(gathered_copies(prefix_keys, "seq", 1))
    masked = jnp.where(keep, scores, neg_value)
    new_peak = jnp.maximum(peak, jnp.max(masked, axis=1))
    expo = jnp.where(keep, jnp.exp(masked - new_peak[:, None]), 0.0)
    peak = new_peak
    total = jnp.sum(expo, axis=1)
    weighted = jnp.sum(expo * dprob, axis=1)
    backward_step = make_backward(peak, total, weighted / total)
    grad_lat, grad_rope, key_grads = backward_step(
        grads_init, gathered_copies(prefix_keys, "seq", 1), jnp.int32(0)
    )
    by_seq = lax.psum_scatter(
        key_grads.astype(jnp.bfloat16), "seq", scatter_dimension=1, tiled=True
    )
    portion = sent_and_summed(by_seq, "head", 1)
    d_keys = of_everyone(portion, "dp")
    dq_lat = (scale * grad_lat).astype(jnp.bfloat16).reshape(tok_rows, heads_here * DL)
    dq_rope = (scale * grad_rope).astype(jnp.bfloat16).reshape(tok_rows, heads_here * DR)
    return (dq_lat, dq_rope, d_keys)


def solution(mesh):
    in_specs = (
        P(("dp", "seq"), "head"),
        P(("dp", "seq"), "head"),
        P(("dp", "seq"), "head"),
        P(None, "seq"),
        P(),
        P(),
    )
    out_specs = (P(("dp", "seq"), "head"), P(("dp", "seq"), "head"), P(None, ("seq", "head")))
    return jax.shard_map(
        on_device, mesh=mesh, in_specs=in_specs, out_specs=out_specs, check_vma=False
    )
```

profile of v0, /device:TPU:2, one launch (start us, length us, event | category | flops | bytes accessed | tf_op | source)
XLA Modules:
  0.0 173.2 jit_solution(10586493975226593176)
XLA Ops:
  7.2 2.7 %broadcast_in_dim.88 = bf16[8,576,256]{2,1,0:T(8,128)(2,1)} broadcast(bf16[576,256]{1,0:T(8,128)(2,1)} %param.9), dimensions={1,2} | broadcast | bytes 2654208 | tf_op jit(solution)/shard_map/broadcast_in_dim | solution.py:17
  9.9 6.0 %all-to-all-start = ((bf16[8,576,256]{2,1,0:T(8,128)(2,1)}), bf16[8,576,256]{2,1,0:T(8,128)(2,1)}, u32[]{:S(2)}, u32[]{:S(2)}) async-start(bf16[8,576,256]{2,1,0:T(8,128)(2,1)} %broadcast_in_dim.88), calls=%async_computation | async-start | bytes 4718592 | tf_op jit(solution)/shard_map/all_to_all | solution.py:16
  16.0 0.3 reshape.68
  16.3 0.9 reshape.69
  17.9 1.2 reshape.72
  19.3 1.1 select_n.47
  20.5 0.2 broadcast_in_dim.97
  20.7 49.9 %all-to-all-done = bf16[8,576,256]{2,1,0:T(8,128)(2,1)} async-done(((bf16[8,576,256]{2,1,0:T(8,128)(2,1)}), bf16[8,576,256]{2,1,0:T(8,128)(2,1)}, u32[]{:S(2)}, u32[]{:S(2)}) %all-to-all-start) | async-done | bytes 2359328 | tf_op jit(solution)/shard_map/all_to_all | solution.py:16
  70.7 3.1 %copy.17 = bf16[8,576,256]{1,2,0:T(8,128)(2,1)S(1)} copy(bf16[8,576,256]{2,1,0:T(8,128)(2,1)} %all-to-all-done) | data formatting | bytes 4718592 | tf_op jit(solution)/shard_map/all_to_all | solution.py:16
  73.8 0.2 slice.18
  74.1 1.8 %fusion.15 = f32[768,2048]{1,0:T(8,128)S(1)} fusion(bf16[768,512]{1,0:T(8,128)(2,1)S(1)} %reshape.68, bf16[512,2048]{0,1:T(8,128)(2,1)S(1)} %bitcast.30), kind=kOutput, calls=%fused_computation.39 | convolution fusion | flops 1610612736 | bytes 9175040 | tf_op jit(solution)/shard_map/dot_general | solution.py:76
  76.0 1.4 fusion.14
  77.3 2.5 %select_reduce_fusion = (f32[768]{0:T(1024)S(1)}, f32[768]{0:T(1024)S(1)}, f32[768,2048]{1,0:T(8,128)S(1)}) fusion(f32[768,2048]{1,0:T(8,128)S(1)} %get-tuple-element.6, f32[768]{0:T(1024)S(1)} %broadcast_maximum_fusion, pred[2048]{0:T(1024)(128)(4,1)S(1)} %iota_compare_fusion.1, bf16[768,512]{1,0:T(8,128)(2,1)S(1)} %copy-done.8, ...), kind=kOutput, calls=%fused_computation.5 | convolution fusion | flops 1618475520 | bytes 15477760 | tf_op jit(solution)/shard_map/dot_general | solution.py:80
  79.9 2.1 %multiply_convert_fusion = bf16[768,2048]{1,0:T(8,128)(2,1)S(1)} fusion(f32[768,2048]{1,0:T(8,128)S(1)} %get-tuple-element.7, f32[768]{0:T(1024)S(1)} %div.33, f32[768]{0:T(1024)S(1)} %get-tuple-element.3, f32[768,2048]{1,0:T(8,128)S(1)} %get-tuple-element.6, f32[768]{0:T(1024)S(1)} %broadcast_maximum_fusion, pred[2048]{0:T(1024)(128)(4,1)S(1)} %iota_compare_fusion.1), kind=kLoop, calls=%fused_computation | loop fusion | flops 9437184 | bytes 15739904 | tf_op jit(solution)/shard_map/convert_element_type | solution.py:94
  82.1 0.7 fusion.4
  82.8 0.4 copy-done.7
  83.2 2.2 %fusion.1 = f32[512,2048]{1,0:T(8,128)S(1)} fusion(bf16[768,512]{1,0:T(8,128)(2,1)S(1)} %copy-done.7, pred[768]{0:T(1024)(128)(4,1)S(1)} %broadcast_in_dim.97, f32[768,2048]{1,0:T(8,128)S(1)} %get-tuple-element.6, f32[768]{0:T(1024)S(1)} %get-tuple-element.3, f32[768]{0:T(1024)S(1)} %broadcast_maximum_fusion, pred[2048]{0:T(1024)(128)(4,1)S(1)} %iota_compare_fusion.1), kind=kOutput, calls=%fused_computation.8 | convolution fusion | flops 1617297408 | bytes 11281152 | tf_op jit(solution)/shard_map/dot_general | solution.py:101
  85.4 2.0 %fusion = bf16[512,2048]{1,0:T(8,128)(2,1)S(1)} fusion(f32[512,2048]{1,0:T(8,128)S(1)} %fusion.1, bf16[768,2048]{1,0:T(8,128)(2,1)S(1)} %multiply_convert_fusion, bf16[768,512]{1,0:T(8,128)(2,1)S(1)} %copy-done.3), kind=kOutput, calls=%fused_computation.7 | convolution fusion | flops 1613758464 | bytes 10223616 | tf_op jit(solution)/shard_map/dot_general | solution.py:103
  87.5 1.7 %pad_maximum_fusion = bf16[576,2048]{1,0:T(8,128)(2,1)} fusion(bf16[64,2048]{1,0:T(8,128)(2,1)S(1)} %fusion.4, bf16[512,2048]{1,0:T(8,128)(2,1)S(1)} %fusion), kind=kLoop, calls=%fused_computation.10 | loop fusion | flops 4718592 | bytes 4718592 | tf_op jit(solution)/shard_map/concatenate | solution.py:109
  89.3 43.9 %reduce-scatter.2.cloned.1.call-done = bf16[576,256]{1,0:T(8,128)(2,1)} async-done(((bf16[576,2048]{1,0:T(8,128)(2,1)}), bf16[576,256]{1,0:T(8,128)(2,1)}) %reduce-scatter.2.cloned.1.call-update) | async-done | bytes 294928 | tf_op jit(solution)/shard_map/reduce_scatter | solution.py:132
  133.2 1.9 %copy.20 = bf16[576,256]{0,1:T(8,128)(2,1)} copy(bf16[576,256]{1,0:T(8,128)(2,1)} %reduce-scatter.2.cloned.1.call-done) | data formatting | bytes 589824 | tf_op jit(solution)/shard_map/reduce_scatter | solution.py:132
  135.0 7.2 %all-to-all-start.1 = ((bf16[8,576,32]{1,2,0:T(8,128)(2,1)}), bf16[8,576,32]{1,2,0:T(8,128)(2,1)S(1)}, u32[]{:S(2)}, u32[]{:S(2)}) async-start(bf16[8,576,32]{1,2,0:T(8,128)(2,1)} %bitcast.35), calls=%async_computation.2 | async-start | bytes 655360 | tf_op jit(solution)/shard_map/all_to_all | solution.py:39
  142.2 4.3 %multiply_convert_fusion.1 = bf16[768,512]{1,0:T(8,128)(2,1)} fusion(bf16[768,2048]{1,0:T(8,128)(2,1)S(1)} %multiply_convert_fusion, bf16[512,2048]{0,1:T(8,128)(2,1)} %bitcast.32), kind=kOutput, calls=%fused_computation.14 | convolution fusion | flops 1611399168 | bytes 6029312 | tf_op jit(solution)/shard_map/dot_general | solution.py:95
  146.5 2.1 %reshape.70 = bf16[384,1024]{1,0:T(8,128)(2,1)} reshape(bf16[768,512]{1,0:T(8,128)(2,1)} %multiply_convert_fusion.1) | data formatting | bytes 1572864 | tf_op jit(solution)/shard_map/reshape | solution.py:137
  148.6 5.9 %all-to-all-done.1 = bf16[8,576,32]{1,2,0:T(8,128)(2,1)S(1)} async-done(((bf16[8,576,32]{1,2,0:T(8,128)(2,1)}), bf16[8,576,32]{1,2,0:T(8,128)(2,1)S(1)}, u32[]{:S(2)}, u32[]{:S(2)}) %all-to-all-start.1) | async-done | bytes 294944 | tf_op jit(solution)/shard_map/all_to_all | solution.py:39
  154.6 0.7 broadcast_in_dim.100
  155.3 4.8 %all-to-all-start.2 = ((f32[4,576,32]{1,2,0:T(8,128)}), f32[4,576,32]{1,2,0:T(8,128)S(1)}, u32[]{:S(2)}, u32[]{:S(2)}) async-start(f32[4,576,32]{1,2,0:T(8,128)} %broadcast_in_dim.100), calls=%async_computation.3 | async-start | bytes 655360 | tf_op jit(solution)/shard_map/all_to_all | solution.py:16
  160.1 2.8 %fusion.5 = bf16[768,64]{0,1:T(8,128)(2,1)} fusion(bf16[768,2048]{1,0:T(8,128)(2,1)S(1)} %multiply_convert_fusion, bf16[64,2048]{0,1:T(8,128)(2,1)} %bitcast.34), kind=kOutput, calls=%fused_computation.16 | convolution fusion | flops 201424896 | bytes 3506176 | tf_op jit(solution)/shard_map/dot_general | solution.py:98
  162.9 1.1 copy.19
  163.9 0.8 reshape.71
  164.7 1.0 all-to-all-done.2
  165.7 0.7 reduce_sum.49
  (33 shorter events, 0.6 us)
Async XLA Ops:
  7.2 8.8 %copy-start.6 = (bf16[384,1024]{1,0:T(8,128)(2,1)S(1)}, bf16[384,1024]{1,0:T(8,128)(2,1)}, u32[]{:S(2)}) copy-start(bf16[384,1024]{1,0:T(8,128)(2,1)} %param.6) | copy-start | bytes 2359300
  7.2 9.1 %copy-start.9 = (bf16[384,128]{1,0:T(8,128)(2,1)S(1)}, bf16[384,128]{1,0:T(8,128)(2,1)}, u32[]{:S(2)}) copy-start(bf16[384,128]{1,0:T(8,128)(2,1)} %param.7) | copy-start | bytes 294916
  7.2 10.7 %copy-start.4 = (bf16[384,1024]{1,0:T(8,128)(2,1)S(1)}, bf16[384,1024]{1,0:T(8,128)(2,1)}, u32[]{:S(2)}) copy-start(bf16[384,1024]{1,0:T(8,128)(2,1)} %param.8) | copy-start | bytes 2359300
  9.9 9.2 %copy-start.10 = (s32[12]{0:T(128)S(1)}, s32[12]{0:T(128)}, u32[]{:S(2)}) copy-start(s32[12]{0:T(128)} %param.10) | copy-start | bytes 148
  9.9 60.8 %all-to-all-start = ((bf16[8,576,256]{2,1,0:T(8,128)(2,1)}), bf16[8,576,256]{2,1,0:T(8,128)(2,1)}, u32[]{:S(2)}, u32[]{:S(2)}) async-start(bf16[8,576,256]{2,1,0:T(8,128)(2,1)} %broadcast_in_dim.88), calls=%async_computation | async-start | bytes 4718592 | tf_op jit(solution)/shard_map/all_to_all | solution.py:16
  15.9 117.3 %reduce-scatter.2.cloned.1.call-start = ((), (), s32[]{:S(2)}) async-start(), calls=%async_computation.4 | async-start | bytes 2654208 | tf_op jit(solution)/shard_map/reduce_scatter | solution.py:132
  16.2 57.8 %copy-start.2 = (bf16[768,512]{1,0:T(8,128)(2,1)}, bf16[768,512]{1,0:T(8,128)(2,1)S(1)}, u32[]{:S(2)}) copy-start(bf16[768,512]{1,0:T(8,128)(2,1)S(1)} %reshape.68) | copy-start | bytes 2359300
  73.9 3.4 %copy-start = (bf16[512,8,256]{0,2,1:T(8,128)(2,1)}, bf16[512,8,256]{0,2,1:T(8,128)(2,1)S(1)}, u32[]{:S(2)}) copy-start(bf16[512,8,256]{0,2,1:T(8,128)(2,1)S(1)} %slice.18) | copy-start | bytes 6291460
  74.1 1.9 %copy-start.1 = (bf16[64,8,256]{0,2,1:T(8,128)(2,1)}, bf16[64,8,256]{0,2,1:T(8,128)(2,1)S(1)}, u32[]{:S(2)}) copy-start(bf16[64,8,256]{0,2,1:T(8,128)(2,1)S(1)} %slice.19) | copy-start | bytes 786436
  74.1 1.9 %copy-start.5 = (bf16[768,64]{1,0:T(8,128)(2,1)S(1)}, bf16[768,64]{1,0:T(8,128)(2,1)}, u32[]{:S(2)}) copy-start(bf16[768,64]{1,0:T(8,128)(2,1)} %reshape.69) | copy-start | bytes 294916
  75.9 1.4 copy-start.8
  82.0 1.1 copy-start.7
  83.2 2.3 %copy-start.3 = (bf16[768,512]{1,0:T(8,128)(2,1)S(1)}, bf16[768,512]{1,0:T(8,128)(2,1)}, u32[]{:S(2)}) copy-start(bf16[768,512]{1,0:T(8,128)(2,1)} %copy-done.2) | copy-start | bytes 2359300
  135.0 19.5 %all-to-all-start.1 = ((bf16[8,576,32]{1,2,0:T(8,128)(2,1)}), bf16[8,576,32]{1,2,0:T(8,128)(2,1)S(1)}, u32[]{:S(2)}, u32[]{:S(2)}) async-start(bf16[8,576,32]{1,2,0:T(8,128)(2,1)} %bitcast.35), calls=%async_computation.2 | async-start | bytes 655360 | tf_op jit(solution)/shard_map/all_to_all | solution.py:39
  155.3 10.4 %all-to-all-start.2 = ((f32[4,576,32]{1,2,0:T(8,128)}), f32[4,576,32]{1,2,0:T(8,128)S(1)}, u32[]{:S(2)}, u32[]{:S(2)}) async-start(f32[4,576,32]{1,2,0:T(8,128)} %broadcast_in_dim.100), calls=%async_computation.3 | async-start | bytes 655360 | tf_op jit(solution)/shard_map/all_to_all | solution.py:16
Sparse Core Ops, SparseCore 0:
  89.4 43.7 reduce-scatter.1
where the time goes:
time: 174 us; the launch traced here: 173 us
  waiting for transfers between devices  101 us (58%)
  starting transfers between devices  18.1 us (10%)
  matrix products  17.8 us (10%)
  local copies, waits for them, and re-layouts  16.8 us (10%)
  between operations  15 us (9%)
  other arithmetic  4.85 us (3%)
    all_to_all x2, waiting for transfers between devices, from_everyone(): lax.all_to_all(jnp.broadcast_to(value[None], (peers, *value.shape)), axis...  50.9 us
    reduce_scatter x1, waiting for transfers between devices, on_device(): lax.psum_scatter(key_grads.astype(jnp.bfloat16), 'seq', scatter_dimension...  43.9 us
    all_to_all x2, starting transfers between devices, from_everyone(): lax.all_to_all(jnp.broadcast_to(value[None], (peers, *value.shape)), axis...  10.8 us
    all_to_all x1, starting transfers between devices, sent_and_summed(): tiles = lax.all_to_all(cut_along(value, dim, peers), axis, 0, 0, tiled=True)  7.2 us
    all_to_all x1, waiting for transfers between devices, sent_and_summed(): tiles = lax.all_to_all(cut_along(value, dim, peers), axis, 0, 0, tiled=True)  5.92 us
    dot_general x1, matrix products, backward_step(): lax.dot_general(dscore_b, key_lat, contract_last, preferred_element_type=...  4.27 us
  transfers between devices with their start and end apart: 4, of which 4 were waited for; matrix products, arithmetic and copies ran while one was open for 9% of the time, Pallas kernels for 0%

commit v1 on v0

v1 whole, which is shorter than its diff:
```python
import jax
import jax.numpy as jnp
from jax import lax
from jax.sharding import PartitionSpec as P

DL = 512
DR = 64
CLEN = 1024
AXES = ("dp", "seq", "head")
NX, NS, NH = 4, 8, 8
NZ = 8
NY = 4

neg_value = -1e30


def moved(dx=0, dy=0, dz=0, dc=0):
    pairs = []
    for x in range(NX):
        for s in range(NS):
            for h in range(NH):
                z = (h % 2) * 4 + s // 2
                tx, ty, tz, tc = (x + dx) % NX, (h // 2 + dy) % NY, (z + dz) % NZ, (s % 2) ^ dc
                src = (x * NS + s) * NH + h
                dst = (tx * NS + (tz % 4) * 2 + tc) * NH + ty * 2 + tz // 4
                pairs.append((src, dst))
    return pairs


def send(value, **shift):
    return lax.ppermute(value, AXES, moved(**shift))


def on_device(q_lat, q_rope, grad_out, prefix_keys, comp_lengths, prefix_len):
    tok_rows = q_lat.shape[0]
    heads_here = q_lat.shape[1] // DL
    rows = tok_rows * heads_here
    width = prefix_keys.shape[1]
    scale = (DL + DR) ** (-0.5)
    seq = lax.axis_index("seq")
    head = lax.axis_index("head")
    core = seq % 2
    zl = seq // 2
    y = head // 2
    zh = head % 2

    half = (DL + DR) // 2
    up_half = send(prefix_keys[:half], dz=2)
    down_half = send(prefix_keys[half:], dz=-2)
    from_below = send(prefix_keys, dz=1)
    from_above = send(prefix_keys, dz=-1)
    opposite = jnp.concatenate([up_half, down_half], axis=0)
    mine = jnp.concatenate([prefix_keys, from_above, from_below, opposite], axis=1)
    other = send(mine, dc=1)
    keys = jnp.concatenate([mine, other], axis=1)

    tok_ids = lax.axis_index(("dp", "seq")) * tok_rows + jnp.arange(tok_rows, dtype=jnp.int32)
    comp_ids = tok_ids // CLEN
    table = jnp.arange(comp_lengths.shape[0], dtype=jnp.int32)
    length = jnp.sum(
        jnp.where(comp_ids[:, None] == table[None, :], comp_lengths[None, :], 0), axis=1
    )
    valid = tok_ids % CLEN < length
    query_lat = q_lat.reshape(rows, DL)
    query_rope = q_rope.reshape(rows, DR)
    upstream = jnp.where(
        jnp.repeat(valid, heads_here)[:, None],
        grad_out.reshape(rows, DL),
        jnp.zeros((), jnp.bfloat16),
    )
    limit = prefix_len[0]

    shard_zl = jnp.array([0, 1, 3, 2], jnp.int32)
    shard_zl = (jnp.tile(shard_zl, 2) + zl) % 4
    shard_c = jnp.repeat(jnp.stack([core, 1 - core]), 4)
    base = (shard_zl * 2 + shard_c) * width
    cols = (base[:, None] + jnp.arange(width, dtype=jnp.int32)[None, :]).reshape(-1)
    keep = (cols < limit)[None, :]

    key_lat = keys[:DL]
    key_rope = keys[DL:]
    scores = (
        jnp.dot(query_lat, key_lat, preferred_element_type=jnp.float32)
        + jnp.dot(query_rope, key_rope, preferred_element_type=jnp.float32)
    ) * scale
    dprob = jnp.dot(upstream, key_lat, preferred_element_type=jnp.float32)
    masked = jnp.where(keep, scores, neg_value)
    peak = jnp.max(masked, axis=1)
    expo = jnp.where(keep, jnp.exp(masked - peak[:, None]), 0.0)
    total = jnp.sum(expo, axis=1)
    delta = jnp.sum(expo * dprob, axis=1) / total
    prob = expo / total[:, None]
    dscore_b = (prob * (dprob - delta[:, None])).astype(jnp.bfloat16)
    prob_b = prob.astype(jnp.bfloat16)

    first = (((0,), (0,)), ((), ()))
    last = (((1,), (1,)), ((), ()))
    term_lat = lax.dot_general(
        prob_b, upstream, first, preferred_element_type=jnp.float32
    ) + scale * lax.dot_general(dscore_b, query_lat, first, preferred_element_type=jnp.float32)
    term_rope = scale * lax.dot_general(
        dscore_b, query_rope, first, preferred_element_type=jnp.float32
    )
    update = jnp.concatenate([term_lat, term_rope], axis=1)
    n = 4 * width
    crossed = send(update[n:].astype(jnp.bfloat16), dc=1)
    chip = (update[:n] + crossed.astype(jnp.float32)).astype(jnp.bfloat16)
    q = width // 2
    opp = chip[3 * width :]
    low = send(opp[:q], dz=2)
    high = send(opp[q:], dz=-2)
    above = send(chip[width : 2 * width], dz=1)
    below = send(chip[2 * width : 3 * width], dz=-1)
    f32 = jnp.float32
    shard = (
        chip[:width].astype(f32)
        + above.astype(f32)
        + below.astype(f32)
        + jnp.concatenate([low, high], axis=0).astype(f32)
    ).astype(jnp.bfloat16)
    part = width // NY

    def slab(k):
        return lax.dynamic_slice_in_dim(shard, ((y + k) % NY) * part, part, 0)

    part_sum = slab(0).astype(f32)
    for k in (1, 3, 2):
        part_sum = part_sum + send(slab(k), dy=k).astype(f32)
    sub = part // 2
    to_send = lax.dynamic_slice_in_dim(part_sum, (1 - zh) * sub, sub, 0).astype(jnp.bfloat16)
    piece = lax.dynamic_slice_in_dim(part_sum, zh * sub, sub, 0) + send(to_send, dz=4).astype(f32)
    whole = piece
    for k in (1, 3, 2):
        whole = whole + send(piece, dx=k)
    d_keys = whole.T

    grad_lat = lax.dot_general(dscore_b, key_lat, last, preferred_element_type=jnp.float32)
    grad_rope = lax.dot_general(dscore_b, key_rope, last, preferred_element_type=jnp.float32)
    dq_lat = (scale * grad_lat).astype(jnp.bfloat16).reshape(tok_rows, heads_here * DL)
    dq_rope = (scale * grad_rope).astype(jnp.bfloat16).reshape(tok_rows, heads_here * DR)
    return (dq_lat, dq_rope, d_keys)


def solution(mesh):
    in_specs = (
        P(("dp", "seq"), "head"),
        P(("dp", "seq"), "head"),
        P(("dp", "seq"), "head"),
        P(None, "seq"),
        P(),
        P(),
    )
    out_specs = (P(("dp", "seq"), "head"), P(("dp", "seq"), "head"), P(None, ("seq", "head")))
    return jax.shard_map(
        on_device, mesh=mesh, in_specs=in_specs, out_specs=out_specs, check_vma=False
    )
```

time: 174 us -> 111 us (0.64)
  the two profiles are of different devices: /device:TPU:2 before, /device:TPU:11 now
where the time goes in v1:
time: 111 us
  waiting for transfers between devices  40.6 us (37%)
  starting transfers between devices  26 us (23%)
  matrix products  18.4 us (17%)
  local copies, waits for them, and re-layouts  14.9 us (13%)
  other arithmetic  9.12 us (8%)
  between operations  1.73 us (2%)
    ppermute x17, waiting for transfers between devices, send(): return lax.ppermute(value, AXES, moved(**shift))  40.6 us
    ppermute x17, starting transfers between devices, send(): return lax.ppermute(value, AXES, moved(**shift))  26 us
    dot_general x1, matrix products, on_device(): lax.dot_general(dscore_b, key_lat, last, preferred_element_type=jnp.float32)  4.31 us
    dot_general x1, matrix products, on_device(): jnp.dot(query_lat, key_lat, preferred_element_type=jnp.float32)  3.02 us
    dot_general x1, matrix products, on_device(): dprob = jnp.dot(upstream, key_lat, preferred_element_type=jnp.float32)  2.85 us
    dot_general x1, matrix products, on_device(): lax.dot_general(prob_b, upstream, first, preferred_element_type=jnp.float32)  2.35 us
    unnamed x26, local copies, waits for them, and re-layouts  2.35 us
  transfers between devices with their start and end apart: 17, of which 8 were waited for; matrix products, arithmetic and copies ran while one was open for 15% of the time, Pallas kernels for 0%

profile of v1, /device:TPU:11, one launch (start us, length us, event | category | flops | bytes accessed | tf_op | source)
XLA Modules:
  0.0 110.7 jit_solution(9936117473259879340)
XLA Ops:
  0.7 5.7 %collective-permute-start = (bf16[576,256]{1,0:T(8,128)(2,1)}, bf16[576,256]{1,0:T(8,128)(2,1)S(1)}, u32[]{:S(2)}, u32[]{:S(2)}) collective-permute-start(bf16[576,256]{1,0:T(8,128)(2,1)} %param.10), channel_id=1, source_target_pairs={{0,49},{1,48},{2,51},{3,50},{4,53},{5,52},{6,55},{7,54},{8,57},{9,... | collective-permute-start | bytes 884744 | tf_op jit(solution)/shard_map/ppermute | solution.py:31
  7.4 3.6 %collective-permute-start.3 = (bf16[288,256]{1,0:T(8,128)(2,1)S(1)}, bf16[288,256]{1,0:T(8,128)(2,1)S(1)}, u32[]{:S(2)}, u32[]{:S(2)}) collective-permute-start(bf16[288,256]{1,0:T(8,128)(2,1)S(1)} %get-tuple-element.19), channel_id=1, source_target_pairs={{0,33},{1,32},{2,35},{3,34},{4,37},{5,36},{6,39},{7,38},{8,41},{9,... | collective-permute-start | bytes 442376 | tf_op jit(solution)/shard_map/ppermute | solution.py:31
  11.0 1.7 %reshape.96 = bf16[768,64]{1,0:T(8,128)(2,1)} reshape(bf16[384,128]{1,0:T(8,128)(2,1)} %param.8) | data formatting | bytes 196608 | tf_op jit(solution)/shard_map/reshape | solution.py:65
  12.7 1.3 %reshape.95 = bf16[768,512]{1,0:T(8,128)(2,1)S(1)} reshape(bf16[384,1024]{1,0:T(8,128)(2,1)} %param.7) | data formatting | bytes 1572864 | tf_op jit(solution)/shard_map/reshape | solution.py:64
  15.2 3.9 %collective-permute-done.2 = bf16[288,256]{1,0:T(8,128)(2,1)S(1)} collective-permute-done((bf16[288,256]{1,0:T(8,128)(2,1)S(1)}, bf16[288,256]{1,0:T(8,128)(2,1)S(1)}, u32[]{:S(2)}, u32[]{:S(2)}) %collective-permute-start.2) | collective-permute-done | bytes 147488 | tf_op jit(solution)/shard_map/ppermute | solution.py:31
  19.1 1.2 %maximum_maximum_fusion = bf16[576,1024]{1,0:T(8,128)(2,1)} fusion(bf16[288,256]{1,0:T(8,128)(2,1)S(1)} %collective-permute-done.3, bf16[288,256]{1,0:T(8,128)(2,1)S(1)} %collective-permute-done.2, bf16[576,256]{1,0:T(8,128)(2,1)S(1)} %collective-permute-done.1, bf16[576,256]{1,0:T(8,128)(2,1)S(1)} %collective-permute-done, bf16[576,256]{1,0:T(8,128)(2,1)S(1)} %copy-done.4), kind=kLoop, calls=%fused_computation.24 | loop fusion | flops 5898240 | bytes 2359296 | tf_op jit(solution)/shard_map/concatenate | solution.py:53
  20.3 2.6 %collective-permute-start.4 = (bf16[576,1024]{1,0:T(8,128)(2,1)}, bf16[576,1024]{1,0:T(8,128)(2,1)S(1)}, u32[]{:S(2)}, u32[]{:S(2)}) collective-permute-start(bf16[576,1024]{1,0:T(8,128)(2,1)} %maximum_maximum_fusion), channel_id=1, source_target_pairs={{0,8},{1,9},{2,10},{3,11},{4,12},{5,13},{6,14},{7,15},{8,0},{9,1},... | collective-permute-start | bytes 3538952 | tf_op jit(solution)/shard_map/ppermute | solution.py:31
  23.0 2.1 %reshape.97 = bf16[768,512]{1,0:T(8,128)(2,1)} reshape(bf16[384,1024]{1,0:T(8,128)(2,1)} %param.9) | data formatting | bytes 1572864 | tf_op jit(solution)/shard_map/reshape | solution.py:68
  27.5 3.0 %fusion.32 = (f32[768]{0:T(1024)S(1)}, f32[2048,768]{1,0:T(8,128)S(1)}) fusion(f32[2048,768]{1,0:T(8,128)S(1)} %fusion.17, bf16[768,512]{1,0:T(8,128)(2,1)S(1)} %reshape.95, bf16[576,2048]{1,0:T(8,128)(2,1)S(1)} %constant_dynamic-update-slice_fusion, pred[2048]{0:T(1024)(128)(4,1)S(1)} %lt.76), kind=kOutput, calls=%fused_computation.73 | convolution fusion | flops 1616903424 | bytes 15471616 | tf_op jit(solution)/shard_map/dot_general | solution.py:83
  31.7 2.9 %fusion = (f32[768]{0:T(1024)S(1)}, f32[768,2048]{0,1:T(8,128)S(1)}) fusion(f32[2048,768]{1,0:T(8,128)S(1)} %get-tuple-element.22, f32[768]{0:T(1024)S(1)} %get-tuple-element.21, pred[2048]{0:T(1024)(128)(4,1)S(1)} %lt.76, bf16[576,2048]{1,0:T(8,128)(2,1)S(1)} %constant_dynamic-update-slice_fusion, bf16[768,512]{1,0:T(8,128)(2,1)S(1)} %copy-done.6, ...), kind=kOutput, calls=%fused_computation.2 | convolution fusion | flops 1617296640 | bytes 15476736 | tf_op jit(solution)/shard_map/dot_general | solution.py:86
  34.6 2.3 %fusion.2 = f32[2048,512]{0,1:T(8,128)S(1)} fusion(bf16[768,512]{1,0:T(8,128)(2,1)S(1)} %copy-done.6, pred[768]{0:T(1024)(128)(4,1)S(1)} %broadcast_in_dim.69, f32[2048,768]{1,0:T(8,128)S(1)} %get-tuple-element.22, f32[768]{0:T(1024)S(1)} %fusion.1, f32[768]{0:T(1024)S(1)} %get-tuple-element.21, pred[2048]{0:T(1024)(128)(4,1)S(1)} %lt.76), kind=kOutput, calls=%fused_computation.10 | convolution fusion | flops 1617297408 | bytes 11281152 | tf_op jit(solution)/shard_map/dot_general | solution.py:98
  36.9 1.9 %multiply_convert_fusion = bf16[768,2048]{0,1:T(8,128)(2,1)S(1)} fusion(f32[768,2048]{0,1:T(8,128)S(1)} %get-tuple-element.24, f32[768]{0:T(1024)S(1)} %div.51, f32[768]{0:T(1024)S(1)} %fusion.1, f32[2048,768]{1,0:T(8,128)S(1)} %get-tuple-element.22, f32[768]{0:T(1024)S(1)} %get-tuple-element.21, pred[2048]{0:T(1024)(128)(4,1)S(1)} %lt.76), kind=kLoop, calls=%fused_computation.4 | loop fusion | flops 9437184 | bytes 15739904 | tf_op jit(solution)/shard_map/convert_element_type | solution.py:93
  40.0 2.1 %multiply_add_fusion = f32[2048,512]{0,1:T(8,128)S(1)} fusion(f32[2048,512]{0,1:T(8,128)S(1)} %fusion.2, bf16[768,2048]{0,1:T(8,128)(2,1)S(1)} %multiply_convert_fusion, bf16[768,512]{1,0:T(8,128)(2,1)S(1)} %copy-done.2), kind=kOutput, calls=%fused_computation.8 | convolution fusion | flops 1612709888 | bytes 12320768 | tf_op jit(solution)/shard_map/dot_general | solution.py:100
  42.4 2.8 %collective-permute-done.5 = bf16[1024,576]{0,1:T(8,128)(2,1)S(1)} collective-permute-done((bf16[1024,576]{0,1:T(8,128)(2,1)S(1)}, bf16[1024,576]{0,1:T(8,128)(2,1)S(1)}, u32[]{:S(2)}, u32[]{:S(2)}) %collective-permute-start.5) | collective-permute-done | bytes 1179680 | tf_op jit(solution)/shard_map/ppermute | solution.py:31
  46.6 1.7 %collective-permute-start.7 = (bf16[256,576]{0,1:T(8,128)(2,1)}, bf16[256,576]{0,1:T(8,128)(2,1)S(1)}, u32[]{:S(2)}, u32[]{:S(2)}) collective-permute-start(bf16[256,576]{0,1:T(8,128)(2,1)} %get-tuple-element.15), channel_id=1, source_target_pairs={{0,49},{1,48},{2,51},{3,50},{4,53},{5,52},{6,55},{7,54},{8,57},{9,... | collective-permute-start | bytes 884744 | tf_op jit(solution)/shard_map/ppermute | solution.py:31
  48.4 1.2 %collective-permute-start.6 = (bf16[256,576]{0,1:T(8,128)(2,1)}, bf16[256,576]{0,1:T(8,128)(2,1)}, u32[]{:S(2)}, u32[]{:S(2)}) collective-permute-start(bf16[256,576]{0,1:T(8,128)(2,1)} %get-tuple-element.14), channel_id=1, source_target_pairs={{0,16},{1,17},{2,18},{3,19},{4,20},{5,21},{6,22},{7,23},{8,24},{9,... | collective-permute-start | bytes 884744 | tf_op jit(solution)/shard_map/ppermute | solution.py:31
  51.5 1.2 %collective-permute-start.8 = (bf16[128,576]{0,1:T(8,128)(2,1)}, bf16[128,576]{0,1:T(8,128)(2,1)}, u32[]{:S(2)}, u32[]{:S(2)}) collective-permute-start(bf16[128,576]{0,1:T(8,128)(2,1)} %get-tuple-element.12), channel_id=1, source_target_pairs={{0,32},{1,33},{2,34},{3,35},{4,36},{5,37},{6,38},{7,39},{8,40},{9,... | collective-permute-start | bytes 442376 | tf_op jit(solution)/shard_map/ppermute | solution.py:31
  52.7 11.6 %collective-permute-done.9 = bf16[128,576]{0,1:T(8,128)(2,1)} collective-permute-done((bf16[128,576]{0,1:T(8,128)(2,1)}, bf16[128,576]{0,1:T(8,128)(2,1)}, u32[]{:S(2)}, u32[]{:S(2)}) %collective-permute-start.9) | collective-permute-done | bytes 147488 | tf_op jit(solution)/shard_map/ppermute | solution.py:31
  65.1 1.4 %add_convert_fusion = bf16[256,576]{0,1:T(8,128)(2,1)S(1)} fusion(bf16[256,576]{0,1:T(8,128)(2,1)} %copy-done.7, bf16[256,576]{0,1:T(8,128)(2,1)} %collective-permute-done.6, bf16[1024,576]{0,1:T(8,128)(2,1)} %copy-done.3, bf16[128,576]{0,1:T(8,128)(2,1)} %collective-permute-done.9, bf16[128,576]{0,1:T(8,128)(2,1)} %collective-permute-done.8), kind=kLoop, calls=%fused_computation.28 | loop fusion | flops 1622016 | bytes 1474560 | tf_op jit(solution)/shard_map/convert_element_type | solution.py:120
  67.4 2.0 %collective-permute-start.12 = (bf16[64,576]{0,1:T(8,128)(2,1)}, bf16[64,576]{0,1:T(8,128)(2,1)}, u32[]{:S(2)}, u32[]{:S(2)}) collective-permute-start(bf16[64,576]{0,1:T(8,128)(2,1)} %get-tuple-element.17), channel_id=1, source_target_pairs={{0,4},{1,5},{2,6},{3,7},{4,0},{5,1},{6,2},{7,3},{8,12},{9,13},{10,... | collective-permute-start | bytes 221192 | tf_op jit(solution)/shard_map/ppermute | solution.py:31
  70.9 2.8 %collective-permute-done.12 = bf16[64,576]{0,1:T(8,128)(2,1)} collective-permute-done((bf16[64,576]{0,1:T(8,128)(2,1)}, bf16[64,576]{0,1:T(8,128)(2,1)}, u32[]{:S(2)}, u32[]{:S(2)}) %collective-permute-start.12) | collective-permute-done | bytes 73760 | tf_op jit(solution)/shard_map/ppermute | solution.py:31
  73.7 4.3 %collective-permute-done.11 = bf16[64,576]{0,1:T(8,128)(2,1)} collective-permute-done((bf16[64,576]{0,1:T(8,128)(2,1)}, bf16[64,576]{0,1:T(8,128)(2,1)}, u32[]{:S(2)}, u32[]{:S(2)}) %collective-permute-start.11) | collective-permute-done | bytes 73760 | tf_op jit(solution)/shard_map/ppermute | solution.py:31
  78.0 1.2 %convert_add_fusion.1 = f32[64,576]{0,1:T(8,128)S(1)} fusion(bf16[64,576]{0,1:T(8,128)(2,1)} %collective-permute-done.12, bf16[64,576]{0,1:T(8,128)(2,1)} %collective-permute-done.11, bf16[64,576]{0,1:T(8,128)(2,1)} %collective-permute-done.10, bf16[256,576]{0,1:T(8,128)(2,1)S(1)} %add_convert_fusion, s32[]{:T(128)S(6)} %select_n.104), kind=kLoop, calls=%fused_computation.32 | loop fusion | flops 258048 | bytes 442372 | tf_op jit(solution)/shard_map/add | solution.py:128
  79.3 1.5 %collective-permute-start.13 = (bf16[32,576]{0,1:T(8,128)(2,1)S(1)}, bf16[32,576]{0,1:T(8,128)(2,1)S(1)}, u32[]{:S(2)}, u32[]{:S(2)}) collective-permute-start(bf16[32,576]{0,1:T(8,128)(2,1)S(1)} %dynamic-slice_convert_fusion), channel_id=1, source_target_pairs={{0,1},{1,0},{2,3},{3,2},{4,5},{5,4},{6,7},{7,6},{8,9},{9,8},{10,11... | collective-permute-start | bytes 110600 | tf_op jit(solution)/shard_map/ppermute | solution.py:31
  80.8 4.3 %multiply_convert_fusion.1 = bf16[768,512]{1,0:T(8,128)(2,1)} fusion(bf16[768,2048]{0,1:T(8,128)(2,1)S(1)} %multiply_convert_fusion, bf16[576,2048]{1,0:T(8,128)(2,1)} %copy-done), kind=kOutput, calls=%fused_computation.23 | convolution fusion | flops 1611399168 | bytes 6029312 | tf_op jit(solution)/shard_map/dot_general | solution.py:137
  85.2 6.2 %collective-permute-done.13 = bf16[32,576]{0,1:T(8,128)(2,1)S(1)} collective-permute-done((bf16[32,576]{0,1:T(8,128)(2,1)S(1)}, bf16[32,576]{0,1:T(8,128)(2,1)S(1)}, u32[]{:S(2)}, u32[]{:S(2)}) %collective-permute-start.13) | collective-permute-done | bytes 36896 | tf_op jit(solution)/shard_map/ppermute | solution.py:31
  91.5 2.2 %collective-permute-start.16 = (f32[32,576]{0,1:T(8,128)S(1)}, f32[32,576]{0,1:T(8,128)}, u32[]{:S(2)}, u32[]{:S(2)}) collective-permute-start(f32[32,576]{0,1:T(8,128)S(1)} %convert_add_fusion), channel_id=1, source_target_pairs={{0,128},{1,129},{2,130},{3,131},{4,132},{5,133},{6,134},{7,135},{8... | collective-permute-start | bytes 221192 | tf_op jit(solution)/shard_map/ppermute | solution.py:31
  93.7 1.2 %collective-permute-start.15 = (f32[32,576]{0,1:T(8,128)S(1)}, f32[32,576]{0,1:T(8,128)}, u32[]{:S(2)}, u32[]{:S(2)}) collective-permute-start(f32[32,576]{0,1:T(8,128)S(1)} %convert_add_fusion), channel_id=1, source_target_pairs={{0,192},{1,193},{2,194},{3,195},{4,196},{5,197},{6,198},{7,199},{8... | collective-permute-start | bytes 221192 | tf_op jit(solution)/shard_map/ppermute | solution.py:31
  95.1 1.6 %fusion.15 = bf16[768,64]{0,1:T(8,128)(2,1)S(1)} fusion(bf16[768,2048]{0,1:T(8,128)(2,1)S(1)} %multiply_convert_fusion, bf16[576,2048]{1,0:T(8,128)(2,1)} %copy-done), kind=kOutput, calls=%fused_computation.26 | convolution fusion | flops 201424896 | bytes 3506176 | tf_op jit(solution)/shard_map/dot_general | solution.py:138
  96.7 2.1 %reshape.98 = bf16[384,1024]{1,0:T(8,128)(2,1)} reshape(bf16[768,512]{1,0:T(8,128)(2,1)} %multiply_convert_fusion.1) | data formatting | bytes 1572864 | tf_op jit(solution)/shard_map/reshape | solution.py:139
  100.7 8.0 %collective-permute-done.15 = f32[32,576]{0,1:T(8,128)} collective-permute-done((f32[32,576]{0,1:T(8,128)S(1)}, f32[32,576]{0,1:T(8,128)}, u32[]{:S(2)}, u32[]{:S(2)}) %collective-permute-start.15) | collective-permute-done | bytes 73760 | tf_op jit(solution)/shard_map/ppermute | solution.py:31
  108.7 1.2 %add_bitcast_fusion = f32[576,32]{1,0:T(8,128)S(1)} fusion(f32[32,576]{0,1:T(8,128)} %collective-permute-done.16, f32[32,576]{0,1:T(8,128)} %collective-permute-done.15, f32[32,576]{0,1:T(8,128)S(1)} %convert_add_fusion, f32[32,576]{0,1:T(8,128)} %collective-permute-done.14), kind=kLoop, calls=%fused_computation.29 | loop fusion | flops 55296 | bytes 368640 | tf_op jit(solution)/shard_map/transpose | solution.py:135
  (72 shorter events, 16.0 us)
Async XLA Ops:
  0.6 14.2 %copy-start.9 = (s32[4]{0:T(128)S(1)}, s32[4]{0:T(128)}, u32[]{:S(2)}) copy-start(s32[4]{0:T(128)} %constant.133.clone) | copy-start | bytes 52
  0.6 18.4 %copy-start.4 = (bf16[576,256]{1,0:T(8,128)(2,1)S(1)}, bf16[576,256]{1,0:T(8,128)(2,1)}, u32[]{:S(2)}) copy-start(bf16[576,256]{1,0:T(8,128)(2,1)} %param.10) | copy-start | bytes 884740
  0.7 18.4 %collective-permute-start = (bf16[576,256]{1,0:T(8,128)(2,1)}, bf16[576,256]{1,0:T(8,128)(2,1)S(1)}, u32[]{:S(2)}, u32[]{:S(2)}) collective-permute-start(bf16[576,256]{1,0:T(8,128)(2,1)} %param.10), channel_id=1, source_target_pairs={{0,49},{1,48},{2,51},{3,50},{4,53},{5,52},{6,55},{7,54},{8,57},{9,... | collective-permute-start | bytes 884744 | tf_op jit(solution)/shard_map/ppermute | solution.py:31
  6.3 12.8 %collective-permute-start.1 = (bf16[576,256]{1,0:T(8,128)(2,1)}, bf16[576,256]{1,0:T(8,128)(2,1)S(1)}, u32[]{:S(2)}, u32[]{:S(2)}) collective-permute-start(bf16[576,256]{1,0:T(8,128)(2,1)} %param.10), channel_id=1, source_target_pairs={{0,16},{1,17},{2,18},{3,19},{4,20},{5,21},{6,22},{7,23},{8,24},{9,... | collective-permute-start | bytes 884744 | tf_op jit(solution)/shard_map/ppermute | solution.py:31
  7.3 11.7 %collective-permute-start.2 = (bf16[288,256]{1,0:T(8,128)(2,1)S(1)}, bf16[288,256]{1,0:T(8,128)(2,1)S(1)}, u32[]{:S(2)}, u32[]{:S(2)}) collective-permute-start(bf16[288,256]{1,0:T(8,128)(2,1)S(1)} %get-tuple-element.20), channel_id=1, source_target_pairs={{0,32},{1,33},{2,34},{3,35},{4,36},{5,37},{6,38},{7,39},{8,40},{9,... | collective-permute-start | bytes 442376 | tf_op jit(solution)/shard_map/ppermute | solution.py:31
  7.4 11.6 %collective-permute-start.3 = (bf16[288,256]{1,0:T(8,128)(2,1)S(1)}, bf16[288,256]{1,0:T(8,128)(2,1)S(1)}, u32[]{:S(2)}, u32[]{:S(2)}) collective-permute-start(bf16[288,256]{1,0:T(8,128)(2,1)S(1)} %get-tuple-element.19), channel_id=1, source_target_pairs={{0,33},{1,32},{2,35},{3,34},{4,37},{5,36},{6,39},{7,38},{8,41},{9,... | collective-permute-start | bytes 442376 | tf_op jit(solution)/shard_map/ppermute | solution.py:31
  14.0 13.4 %copy-start.1 = (bf16[768,512]{1,0:T(8,128)(2,1)}, bf16[768,512]{1,0:T(8,128)(2,1)S(1)}, u32[]{:S(2)}) copy-start(bf16[768,512]{1,0:T(8,128)(2,1)S(1)} %reshape.95) | copy-start | bytes 2359300
  14.1 11.1 %copy-start.8 = (s32[12]{0:T(128)S(1)}, s32[12]{0:T(128)}, u32[]{:S(2)}) copy-start(s32[12]{0:T(128)} %param.11) | copy-start | bytes 148
  20.3 5.4 %collective-permute-start.4 = (bf16[576,1024]{1,0:T(8,128)(2,1)}, bf16[576,1024]{1,0:T(8,128)(2,1)S(1)}, u32[]{:S(2)}, u32[]{:S(2)}) collective-permute-start(bf16[576,1024]{1,0:T(8,128)(2,1)} %maximum_maximum_fusion), channel_id=1, source_target_pairs={{0,8},{1,9},{2,10},{3,11},{4,12},{5,13},{6,14},{7,15},{8,0},{9,1},... | collective-permute-start | bytes 3538952 | tf_op jit(solution)/shard_map/ppermute | solution.py:31
  25.5 0.9 copy-start.5
  26.5 5.2 %copy-start = (bf16[576,2048]{1,0:T(8,128)(2,1)}, bf16[576,2048]{1,0:T(8,128)(2,1)S(1)}, u32[]{:S(2)}) copy-start(bf16[576,2048]{1,0:T(8,128)(2,1)S(1)} %constant_dynamic-update-slice_fusion) | copy-start | bytes 7077892
  30.5 1.2 %copy-start.6 = (bf16[768,512]{1,0:T(8,128)(2,1)S(1)}, bf16[768,512]{1,0:T(8,128)(2,1)}, u32[]{:S(2)}) copy-start(bf16[768,512]{1,0:T(8,128)(2,1)} %reshape.97) | copy-start | bytes 2359300
  38.9 1.1 %copy-start.2 = (bf16[768,512]{1,0:T(8,128)(2,1)S(1)}, bf16[768,512]{1,0:T(8,128)(2,1)}, u32[]{:S(2)}) copy-start(bf16[768,512]{1,0:T(8,128)(2,1)} %copy-done.1) | copy-start | bytes 2359300
  42.3 2.9 %collective-permute-start.5 = (bf16[1024,576]{0,1:T(8,128)(2,1)S(1)}, bf16[1024,576]{0,1:T(8,128)(2,1)S(1)}, u32[]{:S(2)}, u32[]{:S(2)}) collective-permute-start(bf16[1024,576]{0,1:T(8,128)(2,1)S(1)} %fusion.7), channel_id=1, source_target_pairs={{0,8},{1,9},{2,10},{3,11},{4,12},{5,13},{6,14},{7,15},{8,0},{9,1},... | collective-permute-start | bytes 3538952 | tf_op jit(solution)/shard_map/ppermute | solution.py:31
  45.7 3.9 %copy-start.3 = (bf16[1024,576]{0,1:T(8,128)(2,1)}, bf16[1024,576]{0,1:T(8,128)(2,1)S(1)}, u32[]{:S(2)}) copy-start(bf16[1024,576]{0,1:T(8,128)(2,1)S(1)} %fusion.6) | copy-start | bytes 3538948
  46.6 17.7 %collective-permute-start.7 = (bf16[256,576]{0,1:T(8,128)(2,1)}, bf16[256,576]{0,1:T(8,128)(2,1)S(1)}, u32[]{:S(2)}, u32[]{:S(2)}) collective-permute-start(bf16[256,576]{0,1:T(8,128)(2,1)} %get-tuple-element.15), channel_id=1, source_target_pairs={{0,49},{1,48},{2,51},{3,50},{4,53},{5,52},{6,55},{7,54},{8,57},{9,... | collective-permute-start | bytes 884744 | tf_op jit(solution)/shard_map/ppermute | solution.py:31
  48.4 16.7 %collective-permute-start.6 = (bf16[256,576]{0,1:T(8,128)(2,1)}, bf16[256,576]{0,1:T(8,128)(2,1)}, u32[]{:S(2)}, u32[]{:S(2)}) collective-permute-start(bf16[256,576]{0,1:T(8,128)(2,1)} %get-tuple-element.14), channel_id=1, source_target_pairs={{0,16},{1,17},{2,18},{3,19},{4,20},{5,21},{6,22},{7,23},{8,24},{9,... | collective-permute-start | bytes 884744 | tf_op jit(solution)/shard_map/ppermute | solution.py:31
  50.4 14.0 %collective-permute-start.9 = (bf16[128,576]{0,1:T(8,128)(2,1)}, bf16[128,576]{0,1:T(8,128)(2,1)}, u32[]{:S(2)}, u32[]{:S(2)}) collective-permute-start(bf16[128,576]{0,1:T(8,128)(2,1)} %get-tuple-element.13), channel_id=1, source_target_pairs={{0,33},{1,32},{2,35},{3,34},{4,37},{5,36},{6,39},{7,38},{8,41},{9,... | collective-permute-start | bytes 442376 | tf_op jit(solution)/shard_map/ppermute | solution.py:31
  51.5 12.9 %collective-permute-start.8 = (bf16[128,576]{0,1:T(8,128)(2,1)}, bf16[128,576]{0,1:T(8,128)(2,1)}, u32[]{:S(2)}, u32[]{:S(2)}) collective-permute-start(bf16[128,576]{0,1:T(8,128)(2,1)} %get-tuple-element.12), channel_id=1, source_target_pairs={{0,32},{1,33},{2,34},{3,35},{4,36},{5,37},{6,38},{7,39},{8,40},{9,... | collective-permute-start | bytes 442376 | tf_op jit(solution)/shard_map/ppermute | solution.py:31
  64.4 0.7 copy-start.7
  67.4 6.2 %collective-permute-start.12 = (bf16[64,576]{0,1:T(8,128)(2,1)}, bf16[64,576]{0,1:T(8,128)(2,1)}, u32[]{:S(2)}, u32[]{:S(2)}) collective-permute-start(bf16[64,576]{0,1:T(8,128)(2,1)} %get-tuple-element.17), channel_id=1, source_target_pairs={{0,4},{1,5},{2,6},{3,7},{4,0},{5,1},{6,2},{7,3},{8,12},{9,13},{10,... | collective-permute-start | bytes 221192 | tf_op jit(solution)/shard_map/ppermute | solution.py:31
  69.5 8.6 %collective-permute-start.11 = (bf16[64,576]{0,1:T(8,128)(2,1)}, bf16[64,576]{0,1:T(8,128)(2,1)}, u32[]{:S(2)}, u32[]{:S(2)}) collective-permute-start(bf16[64,576]{0,1:T(8,128)(2,1)} %get-tuple-element.18), channel_id=1, source_target_pairs={{0,6},{1,7},{2,0},{3,1},{4,2},{5,3},{6,4},{7,5},{8,14},{9,15},{10,... | collective-permute-start | bytes 221192 | tf_op jit(solution)/shard_map/ppermute | solution.py:31
  70.5 7.5 %collective-permute-start.10 = (bf16[64,576]{0,1:T(8,128)(2,1)}, bf16[64,576]{0,1:T(8,128)(2,1)}, u32[]{:S(2)}, u32[]{:S(2)}) collective-permute-start(bf16[64,576]{0,1:T(8,128)(2,1)} %get-tuple-element.16), channel_id=1, source_target_pairs={{0,2},{1,3},{2,4},{3,5},{4,6},{5,7},{6,0},{7,1},{8,10},{9,11},{10,... | collective-permute-start | bytes 221192 | tf_op jit(solution)/shard_map/ppermute | solution.py:31
  79.3 12.0 %collective-permute-start.13 = (bf16[32,576]{0,1:T(8,128)(2,1)S(1)}, bf16[32,576]{0,1:T(8,128)(2,1)S(1)}, u32[]{:S(2)}, u32[]{:S(2)}) collective-permute-start(bf16[32,576]{0,1:T(8,128)(2,1)S(1)} %dynamic-slice_convert_fusion), channel_id=1, source_target_pairs={{0,1},{1,0},{2,3},{3,2},{4,5},{5,4},{6,7},{7,6},{8,9},{9,8},{10,11... | collective-permute-start | bytes 110600 | tf_op jit(solution)/shard_map/ppermute | solution.py:31
  91.5 9.2 %collective-permute-start.16 = (f32[32,576]{0,1:T(8,128)S(1)}, f32[32,576]{0,1:T(8,128)}, u32[]{:S(2)}, u32[]{:S(2)}) collective-permute-start(f32[32,576]{0,1:T(8,128)S(1)} %convert_add_fusion), channel_id=1, source_target_pairs={{0,128},{1,129},{2,130},{3,131},{4,132},{5,133},{6,134},{7,135},{8... | collective-permute-start | bytes 221192 | tf_op jit(solution)/shard_map/ppermute | solution.py:31
  93.7 15.0 %collective-permute-start.15 = (f32[32,576]{0,1:T(8,128)S(1)}, f32[32,576]{0,1:T(8,128)}, u32[]{:S(2)}, u32[]{:S(2)}) collective-permute-start(f32[32,576]{0,1:T(8,128)S(1)} %convert_add_fusion), channel_id=1, source_target_pairs={{0,192},{1,193},{2,194},{3,195},{4,196},{5,197},{6,198},{7,199},{8... | collective-permute-start | bytes 221192 | tf_op jit(solution)/shard_map/ppermute | solution.py:31
  94.9 13.9 %collective-permute-start.14 = (f32[32,576]{0,1:T(8,128)S(1)}, f32[32,576]{0,1:T(8,128)}, u32[]{:S(2)}, u32[]{:S(2)}) collective-permute-start(f32[32,576]{0,1:T(8,128)S(1)} %convert_add_fusion), channel_id=1, source_target_pairs={{0,64},{1,65},{2,66},{3,67},{4,68},{5,69},{6,70},{7,71},{8,72},{9,... | collective-permute-start | bytes 221192 | tf_op jit(solution)/shard_map/ppermute | solution.py:31

commit v2 on v1

v2 whole, which is shorter than its diff:
```python
import functools
import math

import jax
import jax.numpy as jnp
from jax import lax
from jax.experimental import pallas as pl
from jax.experimental.pallas import tpu as pltpu
from jax.sharding import PartitionSpec as P

DL = 512
DR = 64
DK = DL + DR
CLEN = 1024
LBLK = 128
AXES = ("dp", "seq", "head")
NX, NS, NH = 4, 8, 8
NZ = 8
NY = 4
SCALE = DK ** (-0.5)
LOG2E = math.log2(math.e)
NEG = -1e30
STEPS = (0, 1, 3, 2)

f32 = jnp.float32
bf16 = jnp.bfloat16


def pairs_of(move):
    pairs = []
    for x in range(NX):
        for s in range(NS):
            for h in range(NH):
                z = (h % 2) * 4 + s // 2
                tx, ty, tz, tc = move(x, h // 2, z, s % 2)
                tz = tz % NZ
                src = (x * NS + s) * NH + h
                dst = ((tx % NX) * NS + (tz % 4) * 2 + tc) * NH + (ty % NY) * 2 + tz // 4
                pairs.append((src, dst))
    return pairs


def send(value, dx=0, dy=0, dz=0, dc=0):
    return lax.ppermute(
        value, AXES, pairs_of(lambda x, y, z, c: (x + dx, y + dy, z + dz, c ^ dc))
    )


def send_opposite(value):
    return lax.ppermute(
        value, AXES, pairs_of(lambda x, y, z, c: (x, y, z + 2 if z % 2 == 0 else z - 2, c))
    )


def chunk_bases(info, width):
    bases = []
    for flip in (0, 1):
        for step in STEPS:
            zl = (info[0] + step) % 4
            core = info[1] + flip * (1 - 2 * info[1])
            bases.append((zl * 2 + core) * width)
    return bases


def gradient_kernel(
    info, lens, q_ref, qr_ref, g_ref, k0, k1, k2, k3, k4, k5, k6, k7,
    own_ref, cross_ref, ds_ref,
    s_ref, d_ref, p_ref, gm_ref, qc_ref, gt_ref, qt_ref, m_ref, t_ref, w_ref,
):
    keys = (k0, k1, k2, k3, k4, k5, k6, k7)
    rows = q_ref.shape[0]
    heads = q_ref.shape[1] // DL
    width = k0.shape[1]
    limit = info[3]
    bases = chunk_bases(info, width)
    blocks = rows // LBLK

    for b in range(blocks):
        block = info[2] + b
        start = (block % (CLEN // LBLK)) * LBLK
        length = lens[block // (CLEN // LBLK)]
        row = lax.broadcasted_iota(jnp.int32, (LBLK, DL), 0) + start
        keep_row = row < length
        for h in range(heads):
            tile = g_ref[pl.ds(b * LBLK, LBLK), pl.ds(h * DL, DL)]
            gm_ref[pl.ds(h * rows + b * LBLK, LBLK), :] = jnp.where(
                keep_row, tile.astype(f32), 0.0
            ).astype(bf16)
    for h in range(heads):
        qc_ref[pl.ds(h * rows, rows), pl.ds(0, DL)] = q_ref[:, pl.ds(h * DL, DL)]
        qc_ref[pl.ds(h * rows, rows), pl.ds(DL, DR)] = qr_ref[:, h * DR : (h + 1) * DR]

    for h in range(heads):
        here = pl.ds(h * rows, rows)
        m_ref[...] = jnp.full(m_ref.shape, NEG, f32)
        for c in range(8):

            @pl.when(bases[c] < limit)
            def _(c=c, here=here):
                key = keys[c][...]
                s = jnp.dot(qc_ref[here, :], key, preferred_element_type=f32)
                col = lax.broadcasted_iota(jnp.int32, (1, width), 1) + bases[c]
                s = s * (SCALE * LOG2E) + jnp.where(col < limit, 0.0, NEG)
                s_ref[c] = s
                m_ref[...] = jnp.maximum(
                    m_ref[...], jnp.maximum(s[:, : width // 2], s[:, width // 2 :])
                )
                d_ref[c] = jnp.dot(gm_ref[here, :], key[:DL], preferred_element_type=f32)

        peak = jnp.max(m_ref[...], axis=1, keepdims=True)
        t_ref[...] = jnp.zeros(t_ref.shape, f32)
        w_ref[...] = jnp.zeros(w_ref.shape, f32)
        for c in range(8):

            @pl.when(bases[c] < limit)
            def _(c=c, peak=peak):
                e = jnp.exp2(s_ref[c] - peak)
                s_ref[c] = e
                ed = e * d_ref[c]
                t_ref[...] += e[:, : width // 2] + e[:, width // 2 :]
                w_ref[...] += ed[:, : width // 2] + ed[:, width // 2 :]

        total = jnp.sum(t_ref[...], axis=1, keepdims=True)
        delta = jnp.sum(w_ref[...], axis=1, keepdims=True) / total
        inv = 1.0 / total
        for c in range(8):

            @pl.when(bases[c] < limit)
            def _(c=c, here=here, inv=inv, delta=delta):
                p = s_ref[c] * inv
                p_ref[c, here, :] = p.astype(bf16)
                ds_ref[c, here, :] = (p * (d_ref[c] - delta)).astype(bf16)

    gt_ref[...] = gm_ref[...].T
    qt_ref[...] = qc_ref[...].T
    for c in (4, 5, 6, 7, 3, 1, 2, 0):
        out = own_ref.at[c] if c < 4 else cross_ref.at[c - 4]

        @pl.when(bases[c] < limit)
        def _(c=c, out=out):
            ds = ds_ref[c]
            low = jnp.dot(gt_ref[...], p_ref[c], preferred_element_type=f32)
            full = jnp.dot(qt_ref[...], ds, preferred_element_type=f32) * SCALE
            out[pl.ds(0, DL), :] = (low + full[:DL]).astype(out.dtype)
            out[pl.ds(DL, DR), :] = full[DL:].astype(out.dtype)

        @pl.when(bases[c] >= limit)
        def _(out=out):
            out[...] = jnp.zeros(out.shape, out.dtype)


def query_kernel(info, ds_ref, k0, k1, k2, k3, k4, k5, k6, k7, lat_ref, rope_ref, acc_ref):
    keys = (k0, k1, k2, k3, k4, k5, k6, k7)
    rows = lat_ref.shape[0]
    heads = lat_ref.shape[1] // DL
    width = k0.shape[1]
    bases = chunk_bases(info, width)
    acc_ref[...] = jnp.zeros(acc_ref.shape, f32)
    for c in range(8):

        @pl.when(bases[c] < info[3])
        def _(c=c):
            acc_ref[...] += lax.dot_general(
                ds_ref[c], keys[c][...], (((1,), (1,)), ((), ())), preferred_element_type=f32
            )

    ropes = []
    for h in range(heads):
        part = acc_ref[pl.ds(h * rows, rows), :] * SCALE
        lat_ref[:, pl.ds(h * DL, DL)] = part[:, :DL].astype(bf16)
        ropes.append(part[:, DL:])
    rope_ref[...] = jnp.concatenate(ropes, axis=1).astype(bf16)


def whole(n):
    return [pl.BlockSpec(memory_space=pltpu.VMEM)] * n


def on_device(q_lat, q_rope, grad_out, prefix_keys, comp_lengths, prefix_len):
    rows = q_lat.shape[0]
    heads = q_lat.shape[1] // DL
    width = prefix_keys.shape[1]
    seq = lax.axis_index("seq")
    head = lax.axis_index("head")
    y = head // 2
    zh = head % 2
    first_block = lax.axis_index(("dp", "seq")) * (rows // LBLK)
    info = jnp.stack([seq // 2, seq % 2, first_block, prefix_len[0]]).astype(jnp.int32)

    above = send(prefix_keys, dz=-1)
    below = send(prefix_keys, dz=1)
    opposite = send_opposite(prefix_keys)
    mine = (prefix_keys, above, below, opposite)
    keys = mine + tuple(send(k, dc=1) for k in mine)

    all_rows = rows * heads
    own, cross, ds = pl.pallas_call(
        gradient_kernel,
        out_shape=(
            jax.ShapeDtypeStruct((4, DK, width), f32),
            jax.ShapeDtypeStruct((4, DK, width), bf16),
            jax.ShapeDtypeStruct((8, all_rows, width), bf16),
        ),
        in_specs=[pl.BlockSpec(memory_space=pltpu.SMEM)] * 2 + whole(11),
        out_specs=tuple(whole(3)),
        scratch_shapes=[
            pltpu.VMEM((8, rows, width), f32),
            pltpu.VMEM((8, rows, width), f32),
            pltpu.VMEM((8, all_rows, width), bf16),
            pltpu.VMEM((all_rows, DL), bf16),
            pltpu.VMEM((all_rows, DK), bf16),
            pltpu.VMEM((DL, all_rows), bf16),
            pltpu.VMEM((DK, all_rows), bf16),
            pltpu.VMEM((rows, width // 2), f32),
            pltpu.VMEM((rows, width // 2), f32),
            pltpu.VMEM((rows, width // 2), f32),
        ],
        cost_estimate=pl.CostEstimate(
            flops=8 * all_rows * width * 2 * (DK + DL + DL + DK),
            transcendentals=8 * all_rows * width,
            bytes_accessed=12 << 20,
        ),
        name="prefix_gradient",
    )(info, comp_lengths, q_lat, q_rope, grad_out, *keys)

    crossed = send(cross, dc=1)
    chip = [own[c] + crossed[c].astype(f32) for c in range(4)]
    to_opposite = send_opposite(chip[3].astype(bf16))
    to_above = send(chip[1].astype(bf16), dz=1)
    to_below = send(chip[2].astype(bf16), dz=-1)

    lat, rope = pl.pallas_call(
        query_kernel,
        out_shape=(
            jax.ShapeDtypeStruct((rows, heads * DL), bf16),
            jax.ShapeDtypeStruct((rows, heads * DR), bf16),
        ),
        in_specs=[pl.BlockSpec(memory_space=pltpu.SMEM)] + whole(9),
        out_specs=tuple(whole(2)),
        scratch_shapes=[pltpu.VMEM((all_rows, DK), f32)],
        cost_estimate=pl.CostEstimate(
            flops=8 * all_rows * width * 2 * DK, transcendentals=0, bytes_accessed=7 << 20
        ),
        name="query_gradient",
    )(info, ds, *keys)

    shard = chip[0] + to_above.astype(f32) + to_below.astype(f32) + to_opposite.astype(f32)
    shard = shard.T.astype(bf16)
    part = width // NY

    def slab(k):
        return lax.dynamic_slice_in_dim(shard, ((y + k) % NY) * part, part, 0)

    part_sum = slab(0).astype(f32)
    for k in (1, 3, 2):
        part_sum = part_sum + send(slab(k), dy=k).astype(f32)
    sub = part // 2
    to_send = lax.dynamic_slice_in_dim(part_sum, (1 - zh) * sub, sub, 0).astype(bf16)
    piece = lax.dynamic_slice_in_dim(part_sum, zh * sub, sub, 0) + send(to_send, dz=4).astype(f32)
    summed = piece
    for k in (1, 3, 2):
        summed = summed + send(piece, dx=k)
    return (lat, rope, summed.T)


def solution(mesh):
    in_specs = (
        P(("dp", "seq"), "head"),
        P(("dp", "seq"), "head"),
        P(("dp", "seq"), "head"),
        P(None, "seq"),
        P(),
        P(),
    )
    out_specs = (P(("dp", "seq"), "head"), P(("dp", "seq"), "head"), P(None, ("seq", "head")))
    return jax.shard_map(
        on_device, mesh=mesh, in_specs=in_specs, out_specs=out_specs, check_vma=False
    )
```

time: 111 us -> 103 us (0.928); the launches traced: 111 us -> 101 us
  matrix products: 18.4 us -> 0 us
  waiting for transfers between devices: 40.6 us -> 55.9 us
  Pallas kernels: 0 us -> 14.9 us
  local copies, waits for them, and re-layouts: 14.9 us -> 2.6 us
  other arithmetic: 9.12 us -> 3.77 us
  starting transfers between devices: 26 us -> 22.1 us
    dot_general x8 -> x0, matrix products: 18.4 us -> none  [the longest x1 4.31 us: on_device(): lax.dot_general(dscore_b, key_lat, last, preferred_element_type=jnp.float32)]
    ppermute x17 -> x18, waiting for transfers between devices: 40.6 us -> 55.9 us  [the longest x16 47.2 us: send(): lax.ppermute(value, AXES, pairs_of(lambda x, y, z, c: (x + dx, y + dy, z...]
    pallas_call x0 -> x2, Pallas kernels: none -> 14.9 us  [the longest x1 10.2 us: on_device(): pl.pallas_call(gradient_kernel, out_shape=(jax.ShapeDtypeStruct((4, DK, w...]
    reshape x6 -> x0, local copies, waits for them, and re-layouts: 8.1 us -> none  [the longest x1 2.1 us: on_device(): grad_out.reshape(rows, DL)]
    ppermute x17 -> x18, starting transfers between devices: 26 us -> 22.1 us  [the longest x16 22 us: send(): lax.ppermute(value, AXES, pairs_of(lambda x, y, z, c: (x + dx, y + dy, z...]
    slice x3 -> x0, local copies, waits for them, and re-layouts: 2.7 us -> none  [the longest x1 1.03 us: on_device(): down_half = send(prefix_keys[half:], dz=-2)]
    reduce_sum x2 -> x0, other arithmetic: 1.22 us -> none  [the longest x1 1.13 us: on_device(): total = jnp.sum(expo, axis=1)]
    concatenate x1 -> x0, other arithmetic: 1.2 us -> none  [on_device(): jnp.concatenate([prefix_keys, from_above, from_below, opposite], axis=1)]
  transfers between devices with their start and end apart: 17 -> 18, of which waited for: 8 -> 11; matrix products, arithmetic and copies ran while one was open for 15% -> 1% of each run, Pallas kernels for 0% -> 5%
where the time goes in v2:
time: 103 us; the launch traced here: 101 us
  waiting for transfers between devices  55.9 us (54%)
  starting transfers between devices  22.1 us (21%)
  Pallas kernels  14.9 us (14%)
  other arithmetic  3.77 us (4%)
  local copies, waits for them, and re-layouts  2.6 us (3%)
  between operations  1.41 us (1%)
    ppermute x16, waiting for transfers between devices, send(): lax.ppermute(value, AXES, pairs_of(lambda x, y, z, c: (x + dx, y + dy, z...  47.2 us
    ppermute x16, starting transfers between devices, send(): lax.ppermute(value, AXES, pairs_of(lambda x, y, z, c: (x + dx, y + dy, z...  22 us
    pallas_call x1, Pallas kernels, on_device(): pl.pallas_call(gradient_kernel, out_shape=(jax.ShapeDtypeStruct((4, DK, w...  10.2 us
    ppermute x2, waiting for transfers between devices, send_opposite(): lax.ppermute(value, AXES, pairs_of(lambda x, y, z, c: (x, y, z + 2 if z %...  8.77 us
    pallas_call x1, Pallas kernels, on_device(): pl.pallas_call(query_kernel, out_shape=(jax.ShapeDtypeStruct((rows, heads...  4.68 us
    unnamed x15, local copies, waits for them, and re-layouts  2.29 us
  transfers between devices with their start and end apart: 18, of which 11 were waited for; matrix products, arithmetic and copies ran while one was open for 1% of the time, Pallas kernels for 5%

profile of v2, /device:TPU:11, one launch (start us, length us, event | category | flops | bytes accessed | tf_op | source)
XLA Modules:
  0.0 100.7 jit_solution(1599023649475106260)
XLA Ops:
  0.6 5.7 %collective-permute-start = (bf16[576,256]{1,0:T(8,128)(2,1)}, bf16[576,256]{1,0:T(8,128)(2,1)S(1)}, u32[]{:S(2)}, u32[]{:S(2)}) collective-permute-start(bf16[576,256]{1,0:T(8,128)(2,1)} %k0.3), channel_id=1, source_target_pairs={{0,49},{1,48},{2,51},{3,50},{4,53},{5,52},{6,55},{7,54},{8,57},{9,... | collective-permute-start | bytes 884744 | tf_op jit(solution)/shard_map/ppermute | solution.py:44
  6.3 1.0 collective-permute-start.3
  7.2 11.4 %collective-permute-done.k1 = bf16[576,256]{1,0:T(8,128)(2,1)S(1)} collective-permute-done((bf16[576,256]{1,0:T(8,128)(2,1)}, bf16[576,256]{1,0:T(8,128)(2,1)S(1)}, u32[]{:S(2)}, u32[]{:S(2)}) %collective-permute-start) | collective-permute-done | bytes 294944 | tf_op jit(solution)/shard_map/ppermute | solution.py:44
  18.6 1.5 %collective-permute-start.4 = (bf16[576,256]{1,0:T(8,128)(2,1)S(1)}, bf16[576,256]{1,0:T(8,128)(2,1)S(1)}, u32[]{:S(2)}, u32[]{:S(2)}) collective-permute-start(bf16[576,256]{1,0:T(8,128)(2,1)S(1)} %collective-permute-done.k1), channel_id=1, source_target_pairs={{0,8},{1,9},{2,10},{3,11},{4,12},{5,13},{6,14},{7,15},{8,0},{9,1},... | collective-permute-start | bytes 884744 | tf_op jit(solution)/shard_map/ppermute | solution.py:44
  20.1 3.3 %collective-permute-start.5 = (bf16[576,256]{1,0:T(8,128)(2,1)S(1)}, bf16[576,256]{1,0:T(8,128)(2,1)S(1)}, u32[]{:S(2)}, u32[]{:S(2)}) collective-permute-start(bf16[576,256]{1,0:T(8,128)(2,1)S(1)} %collective-permute-done.1.k2), channel_id=1, source_target_pairs={{0,8},{1,9},{2,10},{3,11},{4,12},{5,13},{6,14},{7,15},{8,0},{9,1},... | collective-permute-start | bytes 884744 | tf_op jit(solution)/shard_map/ppermute | solution.py:44
  24.2 0.6 pad_add_fusion.info
  25.1 0.5 copy-done.3
  25.9 0.7 copy-done.6
  26.6 10.2 %prefix_gradient.1 = (f32[4,576,256]{2,1,0:T(8,128)}, bf16[4,576,256]{2,1,0:T(8,128)(2,1)}, bf16[8,768,256]{2,1,0:T(8,128)(2,1)}) custom-call(s32[4]{0:T(128)} %pad_add_fusion.info, s32[12]{0:T(128)} %lens.1, bf16[384,1024]{1,0:T(8,128)(2,1)} %q_ref.1, bf16[384,128]{1,0:T(8,128)(2,1)} %qr_ref.1, bf16[384,1024]{1,0:T(8,128)(2,1)} %g_ref.1, ...), custom_call_target="tpu_custom_call" | custom-call | flops 6845104128 | bytes 12582912 | tf_op jit(solution)/shard_map/prefix_gradient/pallas_call | solution.py:197
  36.8 0.4 collective-permute-start.7
  37.2 2.7 %collective-permute-done.7 = bf16[4,576,256]{2,1,0:T(8,128)(2,1)S(1)} collective-permute-done((bf16[4,576,256]{2,1,0:T(8,128)(2,1)}, bf16[4,576,256]{2,1,0:T(8,128)(2,1)S(1)}, u32[]{:S(2)}, u32[]{:S(2)}) %collective-permute-start.7) | collective-permute-done | bytes 1179680 | tf_op jit(solution)/shard_map/ppermute | solution.py:44
  39.9 1.6 %fusion.3 = (bf16[576,256]{1,0:T(8,128)(2,1)S(1)}, bf16[576,256]{1,0:T(8,128)(2,1)S(1)}, bf16[576,256]{1,0:T(8,128)(2,1)S(1)}) fusion(f32[4,576,256]{2,1,0:T(8,128)} %get-tuple-element.11, bf16[4,576,256]{2,1,0:T(8,128)(2,1)S(1)} %collective-permute-done.7), kind=kLoop, calls=%fused_computation.7 | loop fusion | flops 1327104 | bytes 3538944 | tf_op jit(solution)/shard_map/convert_element_type | solution.py:229
  41.6 0.5 collective-permute-start.9
  42.0 1.1 %collective-permute-start.8 = (bf16[576,256]{1,0:T(8,128)(2,1)S(1)}, bf16[576,256]{1,0:T(8,128)(2,1)S(1)}, u32[]{:S(2)}, u32[]{:S(2)}) collective-permute-start(bf16[576,256]{1,0:T(8,128)(2,1)S(1)} %get-tuple-element.16), channel_id=1, source_target_pairs={{0,16},{1,17},{2,18},{3,19},{4,20},{5,21},{6,22},{7,23},{8,24},{9,... | collective-permute-start | bytes 884744 | tf_op jit(solution)/shard_map/ppermute | solution.py:44
  43.1 8.8 %collective-permute-done.10 = bf16[576,256]{1,0:T(8,128)(2,1)S(1)} collective-permute-done((bf16[576,256]{1,0:T(8,128)(2,1)S(1)}, bf16[576,256]{1,0:T(8,128)(2,1)S(1)}, u32[]{:S(2)}, u32[]{:S(2)}) %collective-permute-start.10) | collective-permute-done | bytes 294944 | tf_op jit(solution)/shard_map/ppermute | solution.py:50
  51.9 4.6 %collective-permute-done.9 = bf16[576,256]{1,0:T(8,128)(2,1)S(1)} collective-permute-done((bf16[576,256]{1,0:T(8,128)(2,1)S(1)}, bf16[576,256]{1,0:T(8,128)(2,1)S(1)}, u32[]{:S(2)}, u32[]{:S(2)}) %collective-permute-start.9) | collective-permute-done | bytes 294944 | tf_op jit(solution)/shard_map/ppermute | solution.py:44
  56.5 2.5 %collective-permute-done.8 = bf16[576,256]{1,0:T(8,128)(2,1)S(1)} collective-permute-done((bf16[576,256]{1,0:T(8,128)(2,1)S(1)}, bf16[576,256]{1,0:T(8,128)(2,1)S(1)}, u32[]{:S(2)}, u32[]{:S(2)}) %collective-permute-start.8) | collective-permute-done | bytes 294944 | tf_op jit(solution)/shard_map/ppermute | solution.py:44
  58.9 1.2 %fusion.2 = bf16[576,256]{1,0:T(8,128)(2,1)S(1)} fusion(bf16[576,256]{1,0:T(8,128)(2,1)S(1)} %collective-permute-done.10, bf16[576,256]{1,0:T(8,128)(2,1)S(1)} %collective-permute-done.9, bf16[576,256]{1,0:T(8,128)(2,1)S(1)} %collective-permute-done.8, f32[4,576,256]{2,1,0:T(8,128)} %get-tuple-element.11, bf16[4,576,256]{2,1,0:T(8,128)(2,1)S(1)} %collective-permute-done.7), kind=kLoop, calls=%fused_computation.3 | loop fusion | flops 1327104 | bytes 2064384 | tf_op jit(solution)/shard_map/convert_element_type | solution.py:248
  60.4 2.1 %collective-permute-start.13 = (bf16[64,576]{0,1:T(8,128)(2,1)S(1)}, bf16[64,576]{0,1:T(8,128)(2,1)S(1)}, u32[]{:S(2)}, u32[]{:S(2)}) collective-permute-start(bf16[64,576]{0,1:T(8,128)(2,1)S(1)} %get-tuple-element.20), channel_id=1, source_target_pairs={{0,4},{1,5},{2,6},{3,7},{4,0},{5,1},{6,2},{7,3},{8,12},{9,13},{10,... | collective-permute-start | bytes 221192 | tf_op jit(solution)/shard_map/ppermute | solution.py:44
  62.5 1.1 %collective-permute-start.12 = (bf16[64,576]{0,1:T(8,128)(2,1)S(1)}, bf16[64,576]{0,1:T(8,128)(2,1)S(1)}, u32[]{:S(2)}, u32[]{:S(2)}) collective-permute-start(bf16[64,576]{0,1:T(8,128)(2,1)S(1)} %get-tuple-element.21), channel_id=1, source_target_pairs={{0,6},{1,7},{2,0},{3,1},{4,2},{5,3},{6,4},{7,5},{8,14},{9,15},{10,... | collective-permute-start | bytes 221192 | tf_op jit(solution)/shard_map/ppermute | solution.py:44
  63.5 0.4 collective-permute-start.11
  63.9 3.0 %collective-permute-done.13 = bf16[64,576]{0,1:T(8,128)(2,1)S(1)} collective-permute-done((bf16[64,576]{0,1:T(8,128)(2,1)S(1)}, bf16[64,576]{0,1:T(8,128)(2,1)S(1)}, u32[]{:S(2)}, u32[]{:S(2)}) %collective-permute-start.13) | collective-permute-done | bytes 73760 | tf_op jit(solution)/shard_map/ppermute | solution.py:44
  66.9 4.0 %collective-permute-done.12 = bf16[64,576]{0,1:T(8,128)(2,1)S(1)} collective-permute-done((bf16[64,576]{0,1:T(8,128)(2,1)S(1)}, bf16[64,576]{0,1:T(8,128)(2,1)S(1)}, u32[]{:S(2)}, u32[]{:S(2)}) %collective-permute-start.12) | collective-permute-done | bytes 73760 | tf_op jit(solution)/shard_map/ppermute | solution.py:44
  71.1 1.5 %collective-permute-start.14 = (bf16[32,576]{0,1:T(8,128)(2,1)S(1)}, bf16[32,576]{0,1:T(8,128)(2,1)S(1)}, u32[]{:S(2)}, u32[]{:S(2)}) collective-permute-start(bf16[32,576]{0,1:T(8,128)(2,1)S(1)} %dynamic-slice_convert_fusion), channel_id=1, source_target_pairs={{0,1},{1,0},{2,3},{3,2},{4,5},{5,4},{6,7},{7,6},{8,9},{9,8},{10,11... | collective-permute-start | bytes 110600 | tf_op jit(solution)/shard_map/ppermute | solution.py:44
  72.7 10.2 %collective-permute-done.14 = bf16[32,576]{0,1:T(8,128)(2,1)S(1)} collective-permute-done((bf16[32,576]{0,1:T(8,128)(2,1)S(1)}, bf16[32,576]{0,1:T(8,128)(2,1)S(1)}, u32[]{:S(2)}, u32[]{:S(2)}) %collective-permute-start.14) | collective-permute-done | bytes 36896 | tf_op jit(solution)/shard_map/ppermute | solution.py:44
  83.0 1.9 %collective-permute-start.17 = (f32[32,576]{0,1:T(8,128)S(1)}, f32[32,576]{0,1:T(8,128)S(1)}, u32[]{:S(2)}, u32[]{:S(2)}) collective-permute-start(f32[32,576]{0,1:T(8,128)S(1)} %convert_add_fusion), channel_id=1, source_target_pairs={{0,128},{1,129},{2,130},{3,131},{4,132},{5,133},{6,134},{7,135},{8... | collective-permute-start | bytes 221192 | tf_op jit(solution)/shard_map/ppermute | solution.py:44
  84.9 1.2 %collective-permute-start.16 = (f32[32,576]{0,1:T(8,128)S(1)}, f32[32,576]{0,1:T(8,128)S(1)}, u32[]{:S(2)}, u32[]{:S(2)}) collective-permute-start(f32[32,576]{0,1:T(8,128)S(1)} %convert_add_fusion), channel_id=1, source_target_pairs={{0,192},{1,193},{2,194},{3,195},{4,196},{5,197},{6,198},{7,199},{8... | collective-permute-start | bytes 221192 | tf_op jit(solution)/shard_map/ppermute | solution.py:44
  86.1 0.3 collective-permute-start.15
  86.4 4.7 %query_gradient.1 = (bf16[384,1024]{1,0:T(8,128)(2,1)}, bf16[384,128]{1,0:T(8,128)(2,1)}) custom-call(s32[4]{0:T(128)} %pad_add_fusion.info, bf16[8,768,256]{2,1,0:T(8,128)(2,1)} %get-tuple-element.8.ds_ref, bf16[576,256]{1,0:T(8,128)(2,1)} %k0.3, bf16[576,256]{1,0:T(8,128)(2,1)} %copy-done, bf16[576,256]{1,0:T(8,128)(2,1)} %copy-done.1, ...), custom_call_target="tpu_custom_call" | custom-call | flops 1811939328 | bytes 7340032 | tf_op jit(solution)/shard_map/query_gradient/pallas_call | solution.py:232
  91.1 1.6 %collective-permute-done.17 = f32[32,576]{0,1:T(8,128)S(1)} collective-permute-done((f32[32,576]{0,1:T(8,128)S(1)}, f32[32,576]{0,1:T(8,128)S(1)}, u32[]{:S(2)}, u32[]{:S(2)}) %collective-permute-start.17) | collective-permute-done | bytes 73760 | tf_op jit(solution)/shard_map/ppermute | solution.py:44
  92.7 7.1 %collective-permute-done.16 = f32[32,576]{0,1:T(8,128)S(1)} collective-permute-done((f32[32,576]{0,1:T(8,128)S(1)}, f32[32,576]{0,1:T(8,128)S(1)}, u32[]{:S(2)}, u32[]{:S(2)}) %collective-permute-start.16) | collective-permute-done | bytes 73760 | tf_op jit(solution)/shard_map/ppermute | solution.py:44
  99.9 0.8 copy.9
  (29 shorter events, 1.4 us)
Async XLA Ops:
  0.6 18.0 %collective-permute-start = (bf16[576,256]{1,0:T(8,128)(2,1)}, bf16[576,256]{1,0:T(8,128)(2,1)S(1)}, u32[]{:S(2)}, u32[]{:S(2)}) collective-permute-start(bf16[576,256]{1,0:T(8,128)(2,1)} %k0.3), channel_id=1, source_target_pairs={{0,49},{1,48},{2,51},{3,50},{4,53},{5,52},{6,55},{7,54},{8,57},{9,... | collective-permute-start | bytes 884744 | tf_op jit(solution)/shard_map/ppermute | solution.py:44
  6.3 13.9 %collective-permute-start.1 = (bf16[576,256]{1,0:T(8,128)(2,1)}, bf16[576,256]{1,0:T(8,128)(2,1)S(1)}, u32[]{:S(2)}, u32[]{:S(2)}) collective-permute-start(bf16[576,256]{1,0:T(8,128)(2,1)} %k0.3), channel_id=1, source_target_pairs={{0,16},{1,17},{2,18},{3,19},{4,20},{5,21},{6,22},{7,23},{8,24},{9,... | collective-permute-start | bytes 884744 | tf_op jit(solution)/shard_map/ppermute | solution.py:44
  6.3 17.2 %collective-permute-start.2 = (bf16[576,256]{1,0:T(8,128)(2,1)}, bf16[576,256]{1,0:T(8,128)(2,1)S(1)}, u32[]{:S(2)}, u32[]{:S(2)}) collective-permute-start(bf16[576,256]{1,0:T(8,128)(2,1)} %k0.3), channel_id=1, source_target_pairs={{0,32},{1,33},{2,34},{3,35},{4,36},{5,37},{6,38},{7,39},{8,40},{9,... | collective-permute-start | bytes 884744 | tf_op jit(solution)/shard_map/ppermute | solution.py:50
  6.3 18.5 %collective-permute-start.3 = (bf16[576,256]{1,0:T(8,128)(2,1)}, bf16[576,256]{1,0:T(8,128)(2,1)S(1)}, u32[]{:S(2)}, u32[]{:S(2)}) collective-permute-start(bf16[576,256]{1,0:T(8,128)(2,1)} %k0.3), channel_id=1, source_target_pairs={{0,8},{1,9},{2,10},{3,11},{4,12},{5,13},{6,14},{7,15},{8,0},{9,1},... | collective-permute-start | bytes 884744 | tf_op jit(solution)/shard_map/ppermute | solution.py:44
  18.6 6.5 %copy-start = (bf16[576,256]{1,0:T(8,128)(2,1)}, bf16[576,256]{1,0:T(8,128)(2,1)S(1)}, u32[]{:S(2)}) copy-start(bf16[576,256]{1,0:T(8,128)(2,1)S(1)} %collective-permute-done.k1) | copy-start | bytes 884740
  18.6 6.2 %collective-permute-start.4 = (bf16[576,256]{1,0:T(8,128)(2,1)S(1)}, bf16[576,256]{1,0:T(8,128)(2,1)S(1)}, u32[]{:S(2)}, u32[]{:S(2)}) collective-permute-start(bf16[576,256]{1,0:T(8,128)(2,1)S(1)} %collective-permute-done.k1), channel_id=1, source_target_pairs={{0,8},{1,9},{2,10},{3,11},{4,12},{5,13},{6,14},{7,15},{8,0},{9,1},... | collective-permute-start | bytes 884744 | tf_op jit(solution)/shard_map/ppermute | solution.py:44
  20.1 4.9 %copy-start.1 = (bf16[576,256]{1,0:T(8,128)(2,1)}, bf16[576,256]{1,0:T(8,128)(2,1)S(1)}, u32[]{:S(2)}) copy-start(bf16[576,256]{1,0:T(8,128)(2,1)S(1)} %collective-permute-done.1.k2) | copy-start | bytes 884740
  20.1 4.7 %collective-permute-start.5 = (bf16[576,256]{1,0:T(8,128)(2,1)S(1)}, bf16[576,256]{1,0:T(8,128)(2,1)S(1)}, u32[]{:S(2)}, u32[]{:S(2)}) collective-permute-start(bf16[576,256]{1,0:T(8,128)(2,1)S(1)} %collective-permute-done.1.k2), channel_id=1, source_target_pairs={{0,8},{1,9},{2,10},{3,11},{4,12},{5,13},{6,14},{7,15},{8,0},{9,1},... | collective-permute-start | bytes 884744 | tf_op jit(solution)/shard_map/ppermute | solution.py:44
  23.5 1.6 %copy-start.2 = (bf16[576,256]{1,0:T(8,128)(2,1)}, bf16[576,256]{1,0:T(8,128)(2,1)S(1)}, u32[]{:S(2)}) copy-start(bf16[576,256]{1,0:T(8,128)(2,1)S(1)} %collective-permute-done.2.k3) | copy-start | bytes 884740
  23.5 1.6 %collective-permute-start.6 = (bf16[576,256]{1,0:T(8,128)(2,1)S(1)}, bf16[576,256]{1,0:T(8,128)(2,1)S(1)}, u32[]{:S(2)}, u32[]{:S(2)}) collective-permute-start(bf16[576,256]{1,0:T(8,128)(2,1)S(1)} %collective-permute-done.2.k3), channel_id=1, source_target_pairs={{0,8},{1,9},{2,10},{3,11},{4,12},{5,13},{6,14},{7,15},{8,0},{9,1},... | collective-permute-start | bytes 884744 | tf_op jit(solution)/shard_map/ppermute | solution.py:44
  24.8 0.7 copy-start.3
  24.8 0.8 copy-start.4
  24.9 1.0 copy-start.5
  25.8 0.7 copy-start.6
  36.8 3.1 %collective-permute-start.7 = (bf16[4,576,256]{2,1,0:T(8,128)(2,1)}, bf16[4,576,256]{2,1,0:T(8,128)(2,1)S(1)}, u32[]{:S(2)}, u32[]{:S(2)}) collective-permute-start(bf16[4,576,256]{2,1,0:T(8,128)(2,1)} %get-tuple-element.12), channel_id=1, source_target_pairs={{0,8},{1,9},{2,10},{3,11},{4,12},{5,13},{6,14},{7,15},{8,0},{9,1},... | collective-permute-start | bytes 3538952 | tf_op jit(solution)/shard_map/ppermute | solution.py:44
  41.5 10.4 %collective-permute-start.10 = (bf16[576,256]{1,0:T(8,128)(2,1)S(1)}, bf16[576,256]{1,0:T(8,128)(2,1)S(1)}, u32[]{:S(2)}, u32[]{:S(2)}) collective-permute-start(bf16[576,256]{1,0:T(8,128)(2,1)S(1)} %get-tuple-element.17), channel_id=1, source_target_pairs={{0,32},{1,33},{2,34},{3,35},{4,36},{5,37},{6,38},{7,39},{8,40},{9,... | collective-permute-start | bytes 884744 | tf_op jit(solution)/shard_map/ppermute | solution.py:50
  41.6 14.9 %collective-permute-start.9 = (bf16[576,256]{1,0:T(8,128)(2,1)S(1)}, bf16[576,256]{1,0:T(8,128)(2,1)S(1)}, u32[]{:S(2)}, u32[]{:S(2)}) collective-permute-start(bf16[576,256]{1,0:T(8,128)(2,1)S(1)} %get-tuple-element.18), channel_id=1, source_target_pairs={{0,49},{1,48},{2,51},{3,50},{4,53},{5,52},{6,55},{7,54},{8,57},{9,... | collective-permute-start | bytes 884744 | tf_op jit(solution)/shard_map/ppermute | solution.py:44
  42.0 16.9 %collective-permute-start.8 = (bf16[576,256]{1,0:T(8,128)(2,1)S(1)}, bf16[576,256]{1,0:T(8,128)(2,1)S(1)}, u32[]{:S(2)}, u32[]{:S(2)}) collective-permute-start(bf16[576,256]{1,0:T(8,128)(2,1)S(1)} %get-tuple-element.16), channel_id=1, source_target_pairs={{0,16},{1,17},{2,18},{3,19},{4,20},{5,21},{6,22},{7,23},{8,24},{9,... | collective-permute-start | bytes 884744 | tf_op jit(solution)/shard_map/ppermute | solution.py:44
  60.4 6.5 %collective-permute-start.13 = (bf16[64,576]{0,1:T(8,128)(2,1)S(1)}, bf16[64,576]{0,1:T(8,128)(2,1)S(1)}, u32[]{:S(2)}, u32[]{:S(2)}) collective-permute-start(bf16[64,576]{0,1:T(8,128)(2,1)S(1)} %get-tuple-element.20), channel_id=1, source_target_pairs={{0,4},{1,5},{2,6},{3,7},{4,0},{5,1},{6,2},{7,3},{8,12},{9,13},{10,... | collective-permute-start | bytes 221192 | tf_op jit(solution)/shard_map/ppermute | solution.py:44
  62.5 8.4 %collective-permute-start.12 = (bf16[64,576]{0,1:T(8,128)(2,1)S(1)}, bf16[64,576]{0,1:T(8,128)(2,1)S(1)}, u32[]{:S(2)}, u32[]{:S(2)}) collective-permute-start(bf16[64,576]{0,1:T(8,128)(2,1)S(1)} %get-tuple-element.21), channel_id=1, source_target_pairs={{0,6},{1,7},{2,0},{3,1},{4,2},{5,3},{6,4},{7,5},{8,14},{9,15},{10,... | collective-permute-start | bytes 221192 | tf_op jit(solution)/shard_map/ppermute | solution.py:44
  63.5 7.4 %collective-permute-start.11 = (bf16[64,576]{0,1:T(8,128)(2,1)S(1)}, bf16[64,576]{0,1:T(8,128)(2,1)S(1)}, u32[]{:S(2)}, u32[]{:S(2)}) collective-permute-start(bf16[64,576]{0,1:T(8,128)(2,1)S(1)} %get-tuple-element.19), channel_id=1, source_target_pairs={{0,2},{1,3},{2,4},{3,5},{4,6},{5,7},{6,0},{7,1},{8,10},{9,11},{10,... | collective-permute-start | bytes 221192 | tf_op jit(solution)/shard_map/ppermute | solution.py:44
  71.1 11.7 %collective-permute-start.14 = (bf16[32,576]{0,1:T(8,128)(2,1)S(1)}, bf16[32,576]{0,1:T(8,128)(2,1)S(1)}, u32[]{:S(2)}, u32[]{:S(2)}) collective-permute-start(bf16[32,576]{0,1:T(8,128)(2,1)S(1)} %dynamic-slice_convert_fusion), channel_id=1, source_target_pairs={{0,1},{1,0},{2,3},{3,2},{4,5},{5,4},{6,7},{7,6},{8,9},{9,8},{10,11... | collective-permute-start | bytes 110600 | tf_op jit(solution)/shard_map/ppermute | solution.py:44
  83.0 9.7 %collective-permute-start.17 = (f32[32,576]{0,1:T(8,128)S(1)}, f32[32,576]{0,1:T(8,128)S(1)}, u32[]{:S(2)}, u32[]{:S(2)}) collective-permute-start(f32[32,576]{0,1:T(8,128)S(1)} %convert_add_fusion), channel_id=1, source_target_pairs={{0,128},{1,129},{2,130},{3,131},{4,132},{5,133},{6,134},{7,135},{8... | collective-permute-start | bytes 221192 | tf_op jit(solution)/shard_map/ppermute | solution.py:44
  84.9 14.9 %collective-permute-start.16 = (f32[32,576]{0,1:T(8,128)S(1)}, f32[32,576]{0,1:T(8,128)S(1)}, u32[]{:S(2)}, u32[]{:S(2)}) collective-permute-start(f32[32,576]{0,1:T(8,128)S(1)} %convert_add_fusion), channel_id=1, source_target_pairs={{0,192},{1,193},{2,194},{3,195},{4,196},{5,197},{6,198},{7,199},{8... | collective-permute-start | bytes 221192 | tf_op jit(solution)/shard_map/ppermute | solution.py:44
  86.1 13.8 %collective-permute-start.15 = (f32[32,576]{0,1:T(8,128)S(1)}, f32[32,576]{0,1:T(8,128)S(1)}, u32[]{:S(2)}, u32[]{:S(2)}) collective-permute-start(f32[32,576]{0,1:T(8,128)S(1)} %convert_add_fusion), channel_id=1, source_target_pairs={{0,64},{1,65},{2,66},{3,67},{4,68},{5,69},{6,70},{7,71},{8,72},{9,... | collective-permute-start | bytes 221192 | tf_op jit(solution)/shard_map/ppermute | solution.py:44
